TPU v7x, 128 devices: a whole 4x4x4 slice. The times are simulated.
128 devices in a mesh: rows: 32 (over z, y, core), vecs: 4 (over x).
Axes of the slice: x: 4, y: 4, z: 4, core: 2. Of those that a mesh axis runs over, the one named last changes fastest.
Arguments:
- basis: bfloat16 [100, 2097152], P('vecs', 'rows'), may hold values from -6 to 6
- coefficients: bfloat16 [100, 40], replicated, may hold values from -0.625 to 0.625
- eigen_values: float32 [40], P('vecs'), may hold values from -3 to 1
- stiffness: float32 [2097152], P('rows'), may hold values from 6.5 to 10
- damping: float32 [2097152], P('rows'), may hold values from 0.2 to 2
- mass: float32 [2097152], P('rows'), may hold values from 0.5 to 2
- link_count: int32 [32], P('rows'), may hold values from 1024 to 4096, as said below
- lower_cells: int32 [32, 4096], P('rows'), may hold values from 0 to 4095
- upper_cells: int32 [32, 4096], P('rows'), may hold values from 0 to 4095
Outputs:
- eigvecs: bfloat16 [40, 2097152], P('vecs', 'rows')
- residuals: bfloat16 [40, 2097152], P('vecs', 'rows')
- relative_norms: float32 [40], P('vecs')
Inputs may be any that keep to these rules, and one draw needn't show every extreme that they name: Interface s joins subdomain s to subdomain (s + 1) mod 32; only its first link_count[s] slots are used, the others are to be ignored. Some interface uses all 4096 slots in every draw. `lower_cells`: slots beyond link_count[s] hold values that are not used. `upper_cells`: slots beyond link_count[s] hold values that are not used.
All inputs are finite; a program needn't handle non-finite values.
Results may differ from a plain program's by a relative error of at most 0.0037.
The roundings to bfloat16 on the way count: a program that leaves them out, or rounds other values in their place, can miss the bound.
Values may be sent and summed in bfloat16 or wider, within the bound.
A program may use at most 320 MiB of HBM per device.

v0:
```python
import jax
import jax.numpy as jnp
from jax import lax
from jax.sharding import PartitionSpec as P

WID = 64


def from_behind(value, axis, steps):
    count = lax.axis_size(axis)
    pairs = [(source, (source + steps) % count) for source in range(count)]
    return lax.ppermute(value, axis, pairs)


def sent_to_all(value, axis):
    devices = lax.axis_size(axis)
    return lax.all_to_all(
        jnp.broadcast_to(value[None], (devices, *value.shape)), axis, 0, 0, tiled=True
    )


def taken_together(value, axis):
    return sent_to_all(value, axis).sum(axis=0)


def packed_total(arrays, axis):
    vector, at, finished = (jnp.concatenate([a.reshape(-1) for a in arrays]), 0, [])
    subtotal = taken_together(vector, axis)
    for a in arrays:
        finished.append(subtotal[at : at + a.size].reshape(a.shape))
        at += a.size
    return tuple(finished)


def neighbours(values, width_cells):
    depth_pad = jnp.pad(values, ((0, 0), (1, 1), (0, 0)))
    total = depth_pad[:, 2:] + depth_pad[:, :-2]
    across = jnp.pad(values, ((0, 0), (0, 0), (width_cells, width_cells)))
    total = total + across[:, :, 2 * width_cells :] + across[:, :, : -2 * width_cells]
    column = jnp.arange(values.shape[2]) % width_cells
    shifted = jnp.pad(values, ((0, 0), (0, 0), (1, 1)))
    total = total + jnp.where(column < width_cells - 1, shifted[:, :, 2:], 0.0)
    total = total + jnp.where(column > 0, shifted[:, :, :-2], 0.0)
    return total


def on_device(
    basis,
    coefficients,
    eigen_values,
    stiffness,
    damping,
    mass,
    link_count,
    lower_cells,
    upper_cells,
):
    vector_part = eigen_values.shape[0]
    rows_local = basis.shape[1]
    plane_cells = WID * WID
    plane_count = rows_local // plane_cells
    quarter = lax.all_to_all(basis, "vecs", split_axis=1, concat_axis=0, tiled=True)
    quarter_vecs = jnp.dot(coefficients.T, quarter, preferred_element_type=jnp.float32).astype(
        jnp.bfloat16
    )
    eigvecs = lax.all_to_all(quarter_vecs, "vecs", split_axis=0, concat_axis=1, tiled=True)
    vectors = eigvecs.astype(jnp.float32)
    down_lower, down_upper, down_count = from_behind(
        (lower_cells, upper_cells, link_count), "rows", 1
    )
    slot_index = jnp.arange(lower_cells.shape[1], dtype=jnp.int32)
    own_used = slot_index < link_count[0]
    down_used = slot_index < down_count[0]
    planes = eigvecs.reshape(vector_part, plane_count, plane_cells)
    last_plane = planes[:, plane_count - 1, :]
    first_plane = planes[:, 0, :]
    zero_value = jnp.zeros((), jnp.bfloat16)
    send_up = jnp.where(own_used[None, :], last_plane[:, lower_cells[0]], zero_value)
    send_down = jnp.where(down_used[None, :], first_plane[:, down_upper[0]], zero_value)
    from_below = from_behind(send_up, "rows", 1)
    from_above = from_behind(send_down, "rows", -1)
    link_first = (
        jnp.zeros((vector_part, plane_cells), jnp.float32)
        .at[:, down_upper[0]]
        .add(from_below.astype(jnp.float32))
    )
    link_last = (
        jnp.zeros((vector_part, plane_cells), jnp.float32)
        .at[:, lower_cells[0]]
        .add(from_above.astype(jnp.float32))
    )
    link_sum = jnp.zeros((vector_part, plane_count, plane_cells), jnp.float32)
    link_sum = link_sum.at[:, 0, :].add(link_first).at[:, plane_count - 1, :].add(link_last)
    neighbour_sum = neighbours(vectors.reshape(vector_part, plane_count, plane_cells), WID)
    total_coupled = (neighbour_sum + link_sum).reshape(vector_part, rows_local)
    eigen_col = eigen_values[:, None]
    diagonal = (
        eigen_col * eigen_col * mass[None, :] + eigen_col * damping[None, :] + stiffness[None, :]
    )
    coupling = eigen_col * eigen_col * 0.1 + eigen_col * 0.3 + 1.0
    residual_full = diagonal * vectors - coupling * total_coupled
    local_residual = jnp.sum(residual_full * residual_full, axis=1)
    vector_sq, residual_sq = packed_total(
        (jnp.sum(vectors * vectors, axis=1), local_residual), "rows"
    )
    relative_norms = jnp.sqrt(residual_sq) / jnp.sqrt(vector_sq + 1.0)
    return (eigvecs, residual_full.astype(jnp.bfloat16), relative_norms)


def solution(mesh):
    placed = (
        P("vecs", "rows"),
        P(),
        P("vecs"),
        P("rows"),
        P("rows"),
        P("rows"),
        P("rows"),
        P("rows", None),
        P("rows", None),
    )
    return jax.shard_map(
        on_device,
        mesh=mesh,
        in_specs=placed,
        out_specs=(P("vecs", "rows"), P("vecs", "rows"), P("vecs")),
        check_vma=False,
    )
```

profile of v0, /device:TPU:1, one launch (start us, length us, event | category | flops | bytes accessed | tf_op | source)
XLA Modules:
  0.0 387.3 jit_solution(10114052916482525448)
XLA Ops:
  0.6 6.3 %all_to_all.34 = bf16[25,4,16384]{2,1,0:T(4,128)(2,1)S(1)} reshape(bf16[25,65536]{1,0:T(8,128)(2,1)} %param.13) | data formatting | bytes 6553600 | tf_op jit(solution)/shard_map/all_to_all | solution.py:62
  7.0 3.8 copy.53
  10.8 5.0 %all-to-all-start = ((bf16[25,4,16384]{2,0,1:T(8,128)(2,1)}), bf16[25,4,16384]{2,0,1:T(8,128)(2,1)}, u32[]{:S(2)}, u32[]{:S(2)}) async-start(bf16[25,4,16384]{2,0,1:T(8,128)(2,1)} %copy.53), calls=%async_computation | async-start | bytes 8388608 | tf_op jit(solution)/shard_map/all_to_all | solution.py:62
  15.8 2.7 collective-permute-start
  18.6 0.1 collective-permute-start.2
  19.4 0.8 add.120
  20.2 0.8 mul.102
  21.0 0.8 mul.98
  21.8 0.6 fusion.16
  22.4 0.5 add_add_fusion
  23.0 0.6 copy-done.12
  23.6 1.2 iota_compare_fusion
  24.8 39.8 %all-to-all-done = bf16[25,4,16384]{2,0,1:T(8,128)(2,1)} async-done(((bf16[25,4,16384]{2,0,1:T(8,128)(2,1)}), bf16[25,4,16384]{2,0,1:T(8,128)(2,1)}, u32[]{:S(2)}, u32[]{:S(2)}) %all-to-all-start) | async-done | bytes 3276832 | tf_op jit(solution)/shard_map/all_to_all | solution.py:62
  64.6 3.3 all_to_all.37
  67.9 1.9 convolution_convert_fusion
  69.8 3.1 all_to_all.38
  73.0 3.6 all-to-all-start.1
  76.7 24.7 %all-to-all-done.1 = bf16[4,10,16384]{2,1,0:T(8,128)(2,1)S(1)} async-done(((bf16[4,10,16384]{2,1,0:T(8,128)(2,1)}), bf16[4,10,16384]{2,1,0:T(8,128)(2,1)S(1)}, u32[]{:S(2)}, u32[]{:S(2)}) %all-to-all-start.1) | async-done | bytes 1310752 | tf_op jit(solution)/shard_map/all_to_all | solution.py:66
  101.3 10.9 %copy.55 = bf16[10,4,16384]{0,2,1:T(8,128)(2,1)} copy(bf16[10,4,16384]{2,0,1:T(8,128)(2,1)S(1)} %bitcast.40) | data formatting | bytes 2621440 | tf_op jit(solution)/shard_map/all_to_all | solution.py:66
  112.3 2.6 slice_bitcast_fusion
  114.9 15.0 %gather_fusion = bf16[4096,10]{1,0:T(8,128)(2,1)} fusion(bf16[10,4096]{0,1:T(8,128)(2,1)S(1)} %get-tuple-element.30, s32[4096]{0:T(1024)S(1)} %broadcast_clamp_fusion.1), kind=kCustom, calls=%fused_computation | custom fusion | bytes 180224 | tf_op jit(solution)/shard_map/gather | solution.py:78
  130.0 3.4 select_bitcast_fusion.1
  133.3 0.4 copy.56
  133.7 4.3 %collective-permute-start.1 = (bf16[10,4096]{1,0:T(8,128)(2,1)S(1)}, bf16[10,4096]{1,0:T(8,128)(2,1)}, u32[]{:S(2)}, u32[]{:S(2)}) collective-permute-start(bf16[10,4096]{1,0:T(8,128)(2,1)S(1)} %copy.56), channel_id=1, source_target_pairs={{0,4},{4,8},{8,12},{12,16},{16,20},{20,24},{24,28},{28,32},{32,36}... | collective-permute-start | bytes 245768 | tf_op jit(solution)/shard_map/ppermute | solution.py:12
  138.0 12.4 %gather_fusion.1 = bf16[4096,10]{1,0:T(8,128)(2,1)S(1)} fusion(bf16[10,4096]{0,1:T(8,128)(2,1)} %get-tuple-element.29, s32[4096]{0:T(1024)S(1)} %broadcast_clamp_fusion), kind=kCustom, calls=%fused_computation.1 | custom fusion | bytes 180224 | tf_op jit(solution)/shard_map/gather | solution.py:79
  150.4 2.9 select_bitcast_fusion
  153.3 18.2 %convert_element_type.30 = f32[10,16,4096]{0,2,1:T(8,128)} convert(bf16[10,16,4096]{0,2,1:T(8,128)(2,1)} %bitcast.39) | non-fusion elementwise | flops 655360 | bytes 3932160 | tf_op jit(solution)/shard_map/convert_element_type | solution.py:67
  171.5 1.0 copy.54
  172.5 2.3 copy.58
  174.8 0.8 pad.24
  175.6 2.5 copy.66
  178.0 0.9 convert_bitcast_fusion.1
  179.0 2.0 copy.57
  180.9 24.0 %scatter_custom_fusion = f32[10,4096]{0,1:T(8,128)} fusion(s32[4096]{0:T(1024)} %bitcast.49, f32[4096,10]{1,0:T(8,128)} %copy.57, f32[]{:T(128)} %constant.81.clone.1), kind=kCustom, calls=%fused_computation.27 | custom fusion | flops 40960 | bytes 164352 | tf_op jit(solution)/shard_map/scatter-add | solution.py:85
  205.0 12.1 %scatter-add.25 = f32[10,16,4096]{0,2,1:T(8,128)} pad(f32[10,1,4096]{0,2,1:T(8,128)} %bitcast.44, f32[]{:T(128)} %constant.81.clone.1), padding=0_0x0_15x0_0 | pad | bytes 2785284 | tf_op jit(solution)/shard_map/scatter-add | solution.py:93
  217.1 0.9 convert_bitcast_fusion
  218.0 2.0 copy.59
  220.0 24.0 %scatter_custom_fusion.1 = f32[10,4096]{0,1:T(8,128)} fusion(s32[4096]{0:T(1024)} %bitcast.47, f32[4096,10]{1,0:T(8,128)} %copy.59, f32[]{:T(128)} %constant.81.clone.1), kind=kCustom, calls=%fused_computation.25 | custom fusion | flops 40960 | bytes 164352 | tf_op jit(solution)/shard_map/scatter-add | solution.py:90
  244.0 3.0 bitcast_dynamic-update-slice_fusion
  247.0 82.5 %fusion.5 = f32[10,16,4096]{0,2,1:T(8,128)} fusion(f32[10,16,4096]{0,2,1:T(8,128)} %bitcast_dynamic-update-slice_fusion, f32[10,16,4096]{0,2,1:T(8,128)} %convert_element_type.30, pred[4096]{0:T(1024)(128)(4,1)S(1)} %get-tuple-element.33, pred[4096]{0:T(1024)(128)(4,1)S(1)} %copy-done.14), kind=kLoop, calls=%fused_computation.11 | loop fusion | flops 5242880 | bytes 7872512 | tf_op jit(solution)/shard_map/add | solution.py:95
  329.6 19.5 %copy.61 = f32[10,4,16384]{2,0,1:T(8,128)} copy(f32[10,4,16384]{0,2,1:T(8,128)} %bitcast.36) | data formatting | bytes 5242880 | tf_op jit(solution)/shard_map/reshape | solution.py:95
  349.1 3.6 fusion.6
  352.8 0.1 pad_maximum_fusion
  352.9 0.6 broadcast_in_dim.53
  353.5 8.7 %all-to-all-start.2 = ((f32[32,1,20]{2,1,0:T(1,128)}), f32[32,1,20]{2,1,0:T(1,128)S(1)}, u32[]{:S(2)}, u32[]{:S(2)}) async-start(f32[32,1,20]{2,1,0:T(1,128)} %broadcast_in_dim.53), calls=%async_computation.2 | async-start | bytes 32768 | tf_op jit(solution)/shard_map/all_to_all | solution.py:17
  362.2 19.6 %copy.60 = f32[10,65536]{1,0:T(8,128)} copy(f32[10,65536]{0,1:T(8,128)} %bitcast.37) | data formatting | bytes 5242880 | tf_op jit(solution)/shard_map/reshape | solution.py:95
  381.8 4.8 %subtract_convert_fusion = bf16[10,65536]{1,0:T(8,128)(2,1)} fusion(f32[10,65536]{1,0:T(8,128)} %copy.60, bf16[10,65536]{1,0:T(8,128)(2,1)S(1)} %bitcast.43, f32[10]{0:T(128)S(1)} %copy-done.19, f32[65536]{0:T(1024)S(1)} %copy-done.4, f32[65536]{0:T(1024)S(1)} %copy-done.6, f32[10]{0:T(128)S(1)} %copy-done.18, f32[65536]{0:T(1024)S(1)} %copy-done.8, ...), kind=kLoop, calls=%fused_computation.19 | loop fusion | flops 5898240 | bytes 6029432 | tf_op jit(solution)/shard_map/convert_element_type | solution.py:107
  386.7 0.6 rsqrt_multiply_fusion
  (55 shorter events, 0.2 us)
Async XLA Ops:
  0.6 67.3 %copy-start = (bf16[100,40]{0,1:T(8,128)(2,1)S(1)}, bf16[100,40]{0,1:T(8,128)(2,1)}, u32[]{:S(2)}) copy-start(bf16[100,40]{0,1:T(8,128)(2,1)} %param.14) | copy-start | bytes 24004
  10.8 5.0 %copy-start.21 = (s32[1,4096]{1,0:T(1,128)S(1)}, s32[1,4096]{1,0:T(1,128)}, u32[]{:S(2)}) copy-start(s32[1,4096]{1,0:T(1,128)} %param.21) | copy-start | bytes 49156
  10.8 8.6 %copy-start.3 = (f32[65536]{0:T(1024)S(1)}, f32[65536]{0:T(1024)}, u32[]{:S(2)}) copy-start(f32[65536]{0:T(1024)} %param.16) | copy-start | bytes 786436
  10.8 9.4 %copy-start.5 = (f32[65536]{0:T(1024)S(1)}, f32[65536]{0:T(1024)}, u32[]{:S(2)}) copy-start(f32[65536]{0:T(1024)} %param.17) | copy-start | bytes 786436
  10.8 10.2 %copy-start.7 = (f32[65536]{0:T(1024)S(1)}, f32[65536]{0:T(1024)}, u32[]{:S(2)}) copy-start(f32[65536]{0:T(1024)} %param.18) | copy-start | bytes 786436
  10.8 11.6 %copy-start.17 = (f32[10]{0:T(128)S(1)}, f32[10]{0:T(128)}, u32[]{:S(2)}) copy-start(f32[10]{0:T(128)} %param.15) | copy-start | bytes 124
  10.8 12.1 %copy-start.16 = (s32[1,4096]{1,0:T(1,128)S(1)}, s32[1,4096]{1,0:T(1,128)}, u32[]{:S(2)}) copy-start(s32[1,4096]{1,0:T(1,128)} %param.20) | copy-start | bytes 49156
  10.8 53.8 %all-to-all-start = ((bf16[25,4,16384]{2,0,1:T(8,128)(2,1)}), bf16[25,4,16384]{2,0,1:T(8,128)(2,1)}, u32[]{:S(2)}, u32[]{:S(2)}) async-start(bf16[25,4,16384]{2,0,1:T(8,128)(2,1)} %copy.53), calls=%async_computation | async-start | bytes 8388608 | tf_op jit(solution)/shard_map/all_to_all | solution.py:62
  15.8 60.8 %collective-permute-start = (s32[1,4096]{1,0:T(1,128)S(1)}, s32[1,4096]{1,0:T(1,128)S(1)}, u32[]{:S(2)}, u32[]{:S(2)}) collective-permute-start(s32[1,4096]{1,0:T(1,128)S(1)} %copy-done.21), channel_id=1, source_target_pairs={{0,4},{4,8},{8,12},{12,16},{16,20},{20,24},{24,28},{28,32},{32,36}... | collective-permute-start | bytes 49160 | tf_op jit(solution)/shard_map/ppermute | solution.py:12
  18.6 5.0 %collective-permute-start.2 = (s32[1]{0:T(128)}, s32[1]{0:T(128)}, u32[]{:S(2)}, u32[]{:S(2)}) collective-permute-start(s32[1]{0:T(128)} %param.19), channel_id=1, source_target_pairs={{0,4},{4,8},{8,12},{12,16},{16,20},{20,24},{24,28},{28,32},{32,36}... | collective-permute-start | bytes 20 | tf_op jit(solution)/shard_map/ppermute | solution.py:12
  23.0 0.6 copy-start.12
  73.0 28.4 %all-to-all-start.1 = ((bf16[4,10,16384]{2,1,0:T(8,128)(2,1)}), bf16[4,10,16384]{2,1,0:T(8,128)(2,1)S(1)}, u32[]{:S(2)}, u32[]{:S(2)}) async-start(bf16[4,10,16384]{2,1,0:T(8,128)(2,1)} %all_to_all.38), calls=%async_computation.1 | async-start | bytes 4194304 | tf_op jit(solution)/shard_map/all_to_all | solution.py:66
  76.6 35.6 %copy-start.13 = (s32[4096,1]{0,1:T(1,128)}, s32[4096,1]{0,1:T(1,128)S(1)}, u32[]{:S(2)}) copy-start(s32[4096,1]{0,1:T(1,128)S(1)} %compare_select_fusion.1) | copy-start | bytes 49156
  112.3 38.2 %copy-start.15 = (pred[4096]{0:T(1024)(128)(4,1)S(1)}, pred[4096]{0:T(1024)(128)(4,1)}, u32[]{:S(2)}) copy-start(pred[4096]{0:T(1024)(128)(4,1)} %iota_compare_fusion) | copy-start | bytes 12292
  133.7 44.3 %collective-permute-start.1 = (bf16[10,4096]{1,0:T(8,128)(2,1)S(1)}, bf16[10,4096]{1,0:T(8,128)(2,1)}, u32[]{:S(2)}, u32[]{:S(2)}) collective-permute-start(bf16[10,4096]{1,0:T(8,128)(2,1)S(1)} %copy.56), channel_id=1, source_target_pairs={{0,4},{4,8},{8,12},{12,16},{16,20},{20,24},{24,28},{28,32},{32,36}... | collective-permute-start | bytes 245768 | tf_op jit(solution)/shard_map/ppermute | solution.py:12
  174.8 42.3 %collective-permute-start.3 = (bf16[10,4096]{1,0:T(8,128)(2,1)}, bf16[10,4096]{1,0:T(8,128)(2,1)}, u32[]{:S(2)}, u32[]{:S(2)}) collective-permute-start(bf16[10,4096]{1,0:T(8,128)(2,1)} %copy.58), channel_id=1, source_target_pairs={{0,124},{4,0},{8,4},{12,8},{16,12},{20,16},{24,20},{28,24},{32,28}... | collective-permute-start | bytes 245768 | tf_op jit(solution)/shard_map/ppermute | solution.py:12
  218.0 29.1 %copy-start.14 = (pred[4096]{0:T(1024)(128)(4,1)S(1)}, pred[4096]{0:T(1024)(128)(4,1)}, u32[]{:S(2)}) copy-start(pred[4096]{0:T(1024)(128)(4,1)} %get-tuple-element.34) | copy-start | bytes 12292
  329.6 19.5 %copy-start.9 = (f32[4,16384]{1,0:T(4,128)S(1)}, f32[4,16384]{1,0:T(4,128)}, u32[]{:S(2)}) copy-start(f32[4,16384]{1,0:T(4,128)} %add.120) | copy-start | bytes 786436
  329.6 19.5 %copy-start.10 = (f32[4,16384]{1,0:T(4,128)S(1)}, f32[4,16384]{1,0:T(4,128)}, u32[]{:S(2)}) copy-start(f32[4,16384]{1,0:T(4,128)} %mul.102) | copy-start | bytes 786436
  329.6 19.5 %copy-start.11 = (f32[4,16384]{1,0:T(4,128)S(1)}, f32[4,16384]{1,0:T(4,128)}, u32[]{:S(2)}) copy-start(f32[4,16384]{1,0:T(4,128)} %mul.98) | copy-start | bytes 786436
  329.6 19.5 %copy-start.18 = (f32[10]{0:T(128)S(1)}, f32[10]{0:T(128)}, u32[]{:S(2)}) copy-start(f32[10]{0:T(128)} %param.15) | copy-start | bytes 124
  329.6 19.5 %copy-start.19 = (f32[10]{0:T(128)S(1)}, f32[10]{0:T(128)}, u32[]{:S(2)}) copy-start(f32[10]{0:T(128)} %get-tuple-element.31) | copy-start | bytes 124
  329.6 19.5 %copy-start.20 = (f32[10]{0:T(128)S(1)}, f32[10]{0:T(128)}, u32[]{:S(2)}) copy-start(f32[10]{0:T(128)} %get-tuple-element.32) | copy-start | bytes 124
  353.5 33.1 %all-to-all-start.2 = ((f32[32,1,20]{2,1,0:T(1,128)}), f32[32,1,20]{2,1,0:T(1,128)S(1)}, u32[]{:S(2)}, u32[]{:S(2)}) async-start(f32[32,1,20]{2,1,0:T(1,128)} %broadcast_in_dim.53), calls=%async_computation.2 | async-start | bytes 32768 | tf_op jit(solution)/shard_map/all_to_all | solution.py:17
  362.1 19.6 %copy-start.2 = (bf16[2,8,4,16384]{3,1,2,0:T(8,128)(2,1)S(1)}, bf16[2,8,4,16384]{3,1,2,0:T(8,128)(2,1)}, u32[]{:S(2)}) copy-start(bf16[2,8,4,16384]{3,1,2,0:T(8,128)(2,1)} %copy.66) | copy-start | bytes 6291460
  362.2 19.6 %copy-start.4 = (f32[65536]{0:T(1024)S(1)}, f32[65536]{0:T(1024)}, u32[]{:S(2)}) copy-start(f32[65536]{0:T(1024)} %param.16) | copy-start | bytes 786436
  362.2 19.6 %copy-start.6 = (f32[65536]{0:T(1024)S(1)}, f32[65536]{0:T(1024)}, u32[]{:S(2)}) copy-start(f32[65536]{0:T(1024)} %param.17) | copy-start | bytes 786436
  362.2 19.6 %copy-start.8 = (f32[65536]{0:T(1024)S(1)}, f32[65536]{0:T(1024)}, u32[]{:S(2)}) copy-start(f32[65536]{0:T(1024)} %param.18) | copy-start | bytes 786436
  381.8 5.5 %copy-start.1 = (bf16[100,40]{0,1:T(8,128)(2,1)S(1)}, bf16[100,40]{0,1:T(8,128)(2,1)}, u32[]{:S(2)}) copy-start(bf16[100,40]{0,1:T(8,128)(2,1)} %param.14) | copy-start | bytes 24004
where the time goes:
time: 389 us; the launch traced here: 387 us
  other arithmetic  168 us (43%)
  local copies, waits for them, and re-layouts  126 us (32%)
  waiting for transfers between devices  64.5 us (17%)
  starting transfers between devices  24.4 us (6%)
    add x1, other arithmetic, on_device(): total_coupled = (neighbour_sum + link_sum).reshape(vector_part, rows_local)  82.5 us
    all_to_all x1, waiting for transfers between devices, on_device(): lax.all_to_all(basis, 'vecs', split_axis=1, concat_axis=0, tiled=True)  39.8 us
    reshape x2, local copies, waits for them, and re-layouts, on_device(): total_coupled = (neighbour_sum + link_sum).reshape(vector_part, rows_local)  39 us
    all_to_all x1, waiting for transfers between devices, on_device(): lax.all_to_all(quarter_vecs, 'vecs', split_axis=0, concat_axis=1, tiled=T...  24.7 us
    scatter-add x1, other arithmetic, on_device(): link_last = jnp.zeros((vector_part, plane_cells), jnp.float32).at[:, lowe...  24 us
    scatter-add x1, other arithmetic, on_device(): link_first = jnp.zeros((vector_part, plane_cells), jnp.float32).at[:, dow...  24 us
    convert_element_type x1, other arithmetic, on_device(): vectors = eigvecs.astype(jnp.float32)  18.2 us
    scatter-add x2, local copies, waits for them, and re-layouts, on_device(): link_sum.at[:, 0, :].add(link_first).at[:, plane_count - 1, :]  15.1 us
  transfers between devices with their start and end apart: 7, of which 2 were waited for; matrix products, arithmetic and copies ran while one was open for 28% of the time, Pallas kernels for 0%

commit v1 on v0

v1 whole, which is shorter than its diff:
```python
import functools

import jax
import jax.numpy as jnp
from jax import lax
from jax.experimental import pallas as pl
from jax.experimental.pallas import tpu as pltpu
from jax.sharding import PartitionSpec as P

WID = 64
PLANE = WID * WID
SPAN = 1024
SLOTS = 512
LOW = 256


def link_plane(part_a, part_b, gather_ref, scatter_ref, count, link_a, link_b):
    high = PLANE // LOW
    whole = jnp.concatenate(
        [part_a[...].astype(jnp.float32), part_b[...].astype(jnp.float32), jnp.zeros((6, PLANE), jnp.float32)], axis=0
    ).astype(jnp.bfloat16)
    table = jnp.concatenate([whole[:, LOW * h : LOW * (h + 1)] for h in range(high)], axis=0)
    cell = lax.broadcasted_iota(jnp.int32, (LOW, SLOTS), 0)
    slot = lax.broadcasted_iota(jnp.int32, (1, SLOTS), 1)

    def step(t, total):
        at = pl.multiple_of(t * SLOTS, SLOTS)
        source = gather_ref[:, pl.ds(at, SLOTS)]
        target = scatter_ref[:, pl.ds(at, SLOTS)]
        pick = jnp.where(cell == (source & (LOW - 1)), 1.0, 0.0).astype(jnp.bfloat16)
        rows = jnp.dot(table, pick, preferred_element_type=jnp.float32)
        source_high = source >> 8
        value = jnp.zeros((16, SLOTS), jnp.float32)
        for h in range(high):
            value = value + jnp.where(source_high == h, rows[16 * h : 16 * h + 16], 0.0)
        target_high = jnp.where(slot + at < count, target >> 8, -1)
        spread = jnp.concatenate(
            [jnp.where(target_high == h, value, 0.0).astype(jnp.bfloat16) for h in range(high)], axis=0
        )
        place = jnp.where(cell == (target & (LOW - 1)), 1.0, 0.0).astype(jnp.bfloat16)
        return total + lax.dot_general(
            spread, place, (((1,), (1,)), ((), ())), preferred_element_type=jnp.float32
        )

    total = lax.fori_loop(0, PLANE // SLOTS, step, jnp.zeros((16 * high, LOW), jnp.float32))
    for h in range(high):
        link_a[:, LOW * h : LOW * (h + 1)] = total[16 * h : 16 * h + 8]
        link_b[:, LOW * h : LOW * (h + 1)] = total[16 * h + 8 : 16 * h + 10]


def residual_span(ref, out_rows, diag_refs, lam, coupling, z, c, before, after, link, eig_ref, res_ref, sums):
    rows = ref.shape[0]
    base = z * PLANE + c * SPAN
    if not isinstance(base, int):
        base = pl.multiple_of(base, SPAN)

    def load(at, width):
        if not isinstance(at, int):
            at = pl.multiple_of(at, 128)
        return ref[:, pl.ds(at, width)].astype(jnp.float32)

    raw = ref[:, pl.ds(base, SPAN)]
    value = raw.astype(jnp.float32)
    edge = jnp.zeros((rows, 128), jnp.float32)
    left = load(base - 128, 128) if c > 0 else edge
    right = load(base + SPAN, 128) if c < PLANE // SPAN - 1 else edge
    wide = jnp.concatenate([left, value, right], axis=1)
    span = SPAN + 256
    total = pltpu.roll(wide, WID, 1)[:, 128 : 128 + SPAN] + pltpu.roll(wide, span - WID, 1)[:, 128 : 128 + SPAN]
    column = lax.broadcasted_iota(jnp.int32, (1, SPAN), 1) & (WID - 1)
    total = total + jnp.where(column > 0, pltpu.roll(value, 1, 1), 0.0)
    total = total + jnp.where(column < WID - 1, pltpu.roll(value, SPAN - 1, 1), 0.0)
    if before:
        total = total + load(base - PLANE, SPAN)
    if after:
        total = total + load(base + PLANE, SPAN)
    if link is not None:
        total = total + link[:, c * SPAN : (c + 1) * SPAN]
    mass, damping, stiffness = (r[:, pl.ds(base, SPAN)] for r in diag_refs)
    residual = (lam * lam * mass + lam * damping + stiffness) * value - coupling * total
    eig_ref[out_rows, pl.ds(base, SPAN)] = raw
    res_ref[out_rows, pl.ds(base, SPAN)] = residual.astype(jnp.bfloat16)
    vector_sq, residual_sq = sums
    for k in range(SPAN // 128):
        part = slice(128 * k, 128 * (k + 1))
        vector_sq = vector_sq + value[:, part] * value[:, part]
        residual_sq = residual_sq + residual[:, part] * residual[:, part]
    return vector_sq, residual_sq


def residual_all(ea, eb, diag_refs, eigen, links, eig_ref, res_ref, sums_ref):
    depth = ea.shape[1] // PLANE
    for ref, out_rows, link in ((ea, slice(0, 8), 0), (eb, slice(8, 10), 1)):
        lam = eigen[out_rows, :]
        coupling = lam * lam * 0.1 + lam * 0.3 + 1.0
        rows = ref.shape[0]

        def plane(z, sums, before, after, link_ref):
            for c in range(PLANE // SPAN):
                sums = residual_span(
                    ref, out_rows, diag_refs, lam, coupling, z, c, before, after, link_ref, eig_ref, res_ref, sums
                )
            return sums

        zero = jnp.zeros((rows, 128), jnp.float32)
        sums = plane(0, (zero, zero), False, True, links[0][link])
        sums = lax.fori_loop(1, depth - 1, lambda z, s: plane(z, s, True, True, None), sums)
        sums = plane(depth - 1, sums, True, False, links[1][link])
        sums_ref[0, out_rows, :] = sums[0]
        sums_ref[1, out_rows, :] = sums[1]


def finish_kernel(
    ea, eb, above_a, above_b, below_a, below_b, lower, upper, down_lower, down_upper, counts,
    mass, damping, stiffness, eigen, eig_ref, res_ref, sums_ref, first_a, first_b, last_a, last_b,
):
    link_plane(below_a, below_b, down_lower, down_upper, counts[1], first_a, first_b)
    link_plane(above_a, above_b, upper, lower, counts[0], last_a, last_b)
    residual_all(
        ea, eb, (mass, damping, stiffness), eigen, ((first_a, first_b), (last_a, last_b)), eig_ref, res_ref, sums_ref
    )


def finish(*operands):
    rows = operands[0].shape[1]
    vmem = pl.BlockSpec(memory_space=pltpu.VMEM)
    specs = [vmem] * 10 + [pl.BlockSpec(memory_space=pltpu.SMEM)] + [vmem] * 4
    plane = lambda r: pltpu.VMEM((r, PLANE), jnp.float32)
    return pl.pallas_call(
        finish_kernel,
        out_shape=(
            jax.ShapeDtypeStruct((10, rows), jnp.bfloat16),
            jax.ShapeDtypeStruct((10, rows), jnp.bfloat16),
            jax.ShapeDtypeStruct((2, 10, 128), jnp.float32),
        ),
        in_specs=specs,
        out_specs=(vmem, vmem, vmem),
        scratch_shapes=[plane(8), plane(2), plane(8), plane(2)],
        compiler_params=pltpu.CompilerParams(vmem_limit_bytes=40 * 2**20),
        name="finish",
    )(*operands)


def from_behind(value, axis, steps):
    count = lax.axis_size(axis)
    pairs = [(source, (source + steps) % count) for source in range(count)]
    return lax.ppermute(value, axis, pairs)


def on_device(basis, coefficients, eigen_values, stiffness, damping, mass, link_count, lower_cells, upper_cells):
    rows_local = basis.shape[1]
    quarter = lax.all_to_all(basis, "vecs", split_axis=1, concat_axis=0, tiled=True)
    quarter_vecs = jnp.dot(coefficients.T, quarter, preferred_element_type=jnp.float32).astype(jnp.bfloat16)
    eigvecs = lax.all_to_all(quarter_vecs, "vecs", split_axis=0, concat_axis=1, tiled=True)
    lists = jnp.concatenate([lower_cells, upper_cells, jnp.broadcast_to(link_count[:, None], (1, 128))], axis=1)
    down = from_behind(lists, "rows", 1)
    slots = lower_cells.shape[1]
    down_lower, down_upper, down_count = down[:, :slots], down[:, slots : 2 * slots], down[0, 2 * slots :][:1]
    ea, eb = eigvecs[:8], eigvecs[8:]
    below = from_behind(eigvecs[:, rows_local - PLANE :], "rows", 1)
    above = from_behind(eigvecs[:, :PLANE], "rows", -1)
    wide = lambda a: a.reshape(1, rows_local)
    eig, res, sums = finish(
        ea, eb, above[:8], above[8:], below[:8], below[8:], lower_cells, upper_cells, down_lower, down_upper,
        jnp.concatenate([link_count, down_count]), wide(mass), wide(damping), wide(stiffness), eigen_values[:, None],
    )
    local = jnp.sum(sums, axis=2).reshape(1, 20)
    devices = lax.axis_size("rows")
    totals = lax.all_to_all(jnp.broadcast_to(local[None], (devices, 1, 20)), "rows", 0, 0, tiled=True).sum(axis=0)
    totals = totals.reshape(2, 10)
    norms = jnp.sqrt(totals[1]) / jnp.sqrt(totals[0] + 1.0)
    return eig, res, norms


def solution(mesh):
    placed = (
        P("vecs", "rows"), P(), P("vecs"), P("rows"), P("rows"), P("rows"), P("rows"), P("rows", None), P("rows", None),
    )
    return jax.shard_map(
        on_device,
        mesh=mesh,
        in_specs=placed,
        out_specs=(P("vecs", "rows"), P("vecs", "rows"), P("vecs")),
        check_vma=False,
    )
```

time: 389 us -> 145 us (0.37)
  other arithmetic: 168 us -> 1.48 us
  local copies, waits for them, and re-layouts: 126 us -> 20.5 us
  blocking collectives: 0 us -> 16.6 us
  Pallas kernels: 0 us -> 15.3 us
  starting transfers between devices: 24.4 us -> 15.9 us
  waiting for transfers between devices: 64.5 us -> 71.8 us
    add x2 -> x0, other arithmetic: 83.1 us -> none  [the longest x1 82.5 us: on_device(): total_coupled = (neighbour_sum + link_sum).reshape(vector_part, rows_local)]
    scatter-add x2 -> x0, other arithmetic: 48.1 us -> none  [the longest x1 24 us: on_device(): link_last = jnp.zeros((vector_part, plane_cells), jnp.float32).at[:, lowe...]
    reshape x2 -> x0, local copies, waits for them, and re-layouts: 39 us -> none  [on_device(): total_coupled = (neighbour_sum + link_sum).reshape(vector_part, rows_local)]
    gather x2 -> x0, local copies, waits for them, and re-layouts: 27.4 us -> none  [the longest x1 15 us: on_device(): last_plane[:, lower_cells[0]]]
    convert_element_type x4 -> x0, other arithmetic: 24.8 us -> none  [the longest x1 18.2 us: on_device(): vectors = eigvecs.astype(jnp.float32)]
    all_to_all x0 -> x1, blocking collectives: none -> 16.6 us  [on_device(): lax.all_to_all(jnp.broadcast_to(local[None], (devices, 1, 20)), 'rows', 0...]
    pallas_call x0 -> x1, Pallas kernels: none -> 15.3 us  [finish(): pl.pallas_call(finish_kernel, out_shape=(jax.ShapeDtypeStruct((10, rows),...]
    scatter-add x2 -> x0, local copies, waits for them, and re-layouts: 15.1 us -> none  [on_device(): link_sum.at[:, 0, :].add(link_first).at[:, plane_count - 1, :]]
  transfers between devices with their start and end apart: 7 -> 5, of which waited for: 2 -> 5; matrix products, arithmetic and copies ran while one was open for 28% -> 1% of each run, Pallas kernels for 0% -> 0%
where the time goes in v1:
time: 145 us
  waiting for transfers between devices  71.8 us (50%)
  local copies, waits for them, and re-layouts  20.5 us (14%)
  blocking collectives  16.6 us (11%)
  starting transfers between devices  15.9 us (11%)
  Pallas kernels  15.3 us (11%)
  matrix products  1.89 us (1%)
  other arithmetic  1.48 us (1%)
  between operations  1.46 us (1%)
    all_to_all x1, waiting for transfers between devices, on_device(): lax.all_to_all(basis, 'vecs', split_axis=1, concat_axis=0, tiled=True)  48.1 us
    all_to_all x1, waiting for transfers between devices, on_device(): lax.all_to_all(quarter_vecs, 'vecs', split_axis=0, concat_axis=1, tiled=T...  20.1 us
    all_to_all x1, blocking collectives, on_device(): lax.all_to_all(jnp.broadcast_to(local[None], (devices, 1, 20)), 'rows', 0...  16.6 us
    pallas_call x1, Pallas kernels, finish(): pl.pallas_call(finish_kernel, out_shape=(jax.ShapeDtypeStruct((10, rows),...  15.3 us
    all_to_all x3, local copies, waits for them, and re-layouts, on_device(): lax.all_to_all(basis, 'vecs', split_axis=1, concat_axis=0, tiled=True)  13.5 us
    ppermute x3, starting transfers between devices, from_behind(): return lax.ppermute(value, axis, pairs)  7.36 us
    all_to_all x1, starting transfers between devices, on_device(): lax.all_to_all(basis, 'vecs', split_axis=1, concat_axis=0, tiled=True)  4.84 us
    all_to_all x2, local copies, waits for them, and re-layouts, on_device(): lax.all_to_all(quarter_vecs, 'vecs', split_axis=0, concat_axis=1, tiled=T...  4.16 us
  transfers between devices with their start and end apart: 5, of which 5 were waited for; matrix products, arithmetic and copies ran while one was open for 1% of the time, Pallas kernels for 0%

profile of v1, /device:TPU:1, one launch (start us, length us, event | category | flops | bytes accessed | tf_op | source)
XLA Modules:
  0.0 145.0 jit_solution(12327578682805874888)
XLA Ops:
  0.6 0.0 copy-start
  0.6 6.3 %all_to_all.31 = bf16[25,4,16384]{2,1,0:T(4,128)(2,1)S(1)} reshape(bf16[25,65536]{1,0:T(8,128)(2,1)} %param.9) | data formatting | bytes 6553600 | tf_op jit(solution)/shard_map/all_to_all | solution.py:152
  7.0 3.8 %copy.24 = bf16[25,4,16384]{2,0,1:T(8,128)(2,1)} copy(bf16[25,4,16384]{2,1,0:T(4,128)(2,1)S(1)} %all_to_all.31) | data formatting | bytes 6553600 | tf_op jit(solution)/shard_map/all_to_all | solution.py:152
  10.8 4.8 %all-to-all-start = ((bf16[25,4,16384]{2,0,1:T(8,128)(2,1)}), bf16[25,4,16384]{2,0,1:T(8,128)(2,1)}, u32[]{:S(2)}, u32[]{:S(2)}) async-start(bf16[25,4,16384]{2,0,1:T(8,128)(2,1)} %copy.24), calls=%async_computation | async-start | bytes 8388608 | tf_op jit(solution)/shard_map/all_to_all | solution.py:152
  16.3 48.1 %all-to-all-done = bf16[25,4,16384]{2,0,1:T(8,128)(2,1)} async-done(((bf16[25,4,16384]{2,0,1:T(8,128)(2,1)}), bf16[25,4,16384]{2,0,1:T(8,128)(2,1)}, u32[]{:S(2)}, u32[]{:S(2)}) %all-to-all-start) | async-done | bytes 3276832 | tf_op jit(solution)/shard_map/all_to_all | solution.py:152
  64.4 3.3 %all_to_all.34 = bf16[100,16384]{1,0:T(8,128)(2,1)S(1)} reshape(bf16[4,25,16384]{2,1,0:T(8,128)(2,1)} %bitcast) | data formatting | bytes 6553600 | tf_op jit(solution)/shard_map/all_to_all | solution.py:152
  67.8 0.0 copy-done
  67.8 1.9 %convolution_convert_fusion = bf16[40,16384]{1,0:T(8,128)(2,1)} fusion(bf16[100,40]{0,1:T(8,128)(2,1)S(1)} %copy-done, bf16[100,16384]{1,0:T(8,128)(2,1)S(1)} %all_to_all.34), kind=kOutput, calls=%fused_computation | convolution fusion | flops 131727360 | bytes 4595520 | tf_op jit(solution)/shard_map/dot_general | solution.py:153
  69.7 3.1 %all_to_all.35 = bf16[4,10,16384]{2,1,0:T(8,128)(2,1)} reshape(bf16[40,16384]{1,0:T(8,128)(2,1)} %convolution_convert_fusion) | data formatting | bytes 2621440 | tf_op jit(solution)/shard_map/all_to_all | solution.py:154
  72.8 0.0 copy-start.4
  72.8 0.0 copy-start.5
  72.8 0.0 copy-start.6
  72.8 3.7 %all-to-all-start.1 = ((bf16[4,10,16384]{2,1,0:T(8,128)(2,1)}), bf16[4,10,16384]{2,1,0:T(8,128)(2,1)S(1)}, u32[]{:S(2)}, u32[]{:S(2)}) async-start(bf16[4,10,16384]{2,1,0:T(8,128)(2,1)} %all_to_all.35), calls=%async_computation.1 | async-start | bytes 4194304 | tf_op jit(solution)/shard_map/all_to_all | solution.py:154
  76.6 0.0 copy-done.4
  76.6 0.0 copy-done.5
  76.6 3.1 %collective-permute-start.2 = (s32[1,8320]{1,0:T(1,128)S(1)}, s32[1,8320]{1,0:T(1,128)S(1)}, u32[]{:S(2)}, u32[]{:S(2)}) collective-permute-start(s32[1,8320]{1,0:T(1,128)S(1)} %reshape_add_fusion), channel_id=1, source_target_pairs={{0,4},{4,8},{8,12},{12,16},{16,20},{20,24},{24,28},{28,32},{32,36}... | collective-permute-start | bytes 99848 | tf_op jit(solution)/shard_map/ppermute | solution.py:147
  79.7 0.0 copy-done.6
  79.7 0.1 copy.26.eigen
  79.8 0.9 collective-permute-done.2
  80.7 0.5 slice.78
  81.3 20.1 %all-to-all-done.1 = bf16[4,10,16384]{2,1,0:T(8,128)(2,1)S(1)} async-done(((bf16[4,10,16384]{2,1,0:T(8,128)(2,1)}), bf16[4,10,16384]{2,1,0:T(8,128)(2,1)S(1)}, u32[]{:S(2)}, u32[]{:S(2)}) %all-to-all-start.1) | async-done | bytes 1310752 | tf_op jit(solution)/shard_map/all_to_all | solution.py:154
  101.3 1.0 copy.25
  102.4 0.8 pad.5
  103.1 1.2 copy.29
  104.3 0.0 copy-start.1
  104.3 0.0 copy-start.2
  104.3 0.0 copy-start.3
  104.3 2.5 %collective-permute-start = (bf16[10,4096]{1,0:T(8,128)(2,1)S(1)}, bf16[10,4096]{1,0:T(8,128)(2,1)S(1)}, u32[]{:S(2)}, u32[]{:S(2)}) collective-permute-start(bf16[10,4096]{1,0:T(8,128)(2,1)S(1)} %get-tuple-element.10), channel_id=1, source_target_pairs={{0,124},{4,0},{8,4},{12,8},{16,12},{20,16},{24,20},{28,24},{32,28}... | collective-permute-start | bytes 245768 | tf_op jit(solution)/shard_map/ppermute | solution.py:147
  106.9 1.7 %collective-permute-start.1 = (bf16[10,4096]{1,0:T(8,128)(2,1)S(1)}, bf16[10,4096]{1,0:T(8,128)(2,1)S(1)}, u32[]{:S(2)}, u32[]{:S(2)}) collective-permute-start(bf16[10,4096]{1,0:T(8,128)(2,1)S(1)} %get-tuple-element.9), channel_id=1, source_target_pairs={{0,4},{4,8},{8,12},{12,16},{16,20},{20,24},{24,28},{28,32},{32,36}... | collective-permute-start | bytes 245768 | tf_op jit(solution)/shard_map/ppermute | solution.py:147
  108.6 0.7 pad_add_fusion.counts
  109.3 0.1 slice.68
  109.4 0.1 slice.69
  109.6 1.5 %collective-permute-done = bf16[10,4096]{1,0:T(8,128)(2,1)S(1)} collective-permute-done((bf16[10,4096]{1,0:T(8,128)(2,1)S(1)}, bf16[10,4096]{1,0:T(8,128)(2,1)S(1)}, u32[]{:S(2)}, u32[]{:S(2)}) %collective-permute-start) | collective-permute-done | bytes 81952 | tf_op jit(solution)/shard_map/ppermute | solution.py:147
  111.0 1.2 collective-permute-done.1
  112.3 0.0 copy-done.1
  112.3 0.0 copy-done.2
  112.3 0.0 copy-done.3
  112.3 15.3 %finish.1 = (bf16[10,65536]{1,0:T(8,128)(2,1)}, bf16[10,65536]{1,0:T(8,128)(2,1)}, f32[2,10,128]{2,1,0:T(8,128)S(1)}) custom-call(bf16[8,65536]{1,0:T(8,128)(2,1)S(1)} %bitcast.19, bf16[2,65536]{1,0:T(2,128)(2,1)S(1)} %bitcast.20, bf16[8,4096]{1,0:T(8,128)(2,1)S(1)} %slice.71.above_a, bf16[2,4096]{1,0:T(2,128)(2,1)S(1)} %slice.72.above_b, ...), custom_call_target="tpu_custom_call" | custom-call | tf_op jit(solution)/shard_map/finish/pallas_call | solution.py:129
  127.6 0.1 reduce_sum.20
  127.7 0.1 broadcast_in_dim.21
  127.8 16.6 %all_to_all.43 = f32[32,1,20]{2,1,0:T(1,128)S(1)} all-to-all(f32[32,1,20]{2,1,0:T(1,128)S(1)} %broadcast_in_dim.22), channel_id=1, replica_groups=mesh['rows'=32,'vecs'=4] {'rows'}, dimensions={0} | all-to-all | bytes 5120 | tf_op jit(solution)/shard_map/all_to_all | solution.py:169
  144.4 0.1 reduce_sum.21
  144.4 0.6 multiply_bitcast_fusion
  (10 shorter events, 0.1 us)
Async XLA Ops:
  0.6 67.1 %copy-start = (bf16[100,40]{0,1:T(8,128)(2,1)S(1)}, bf16[100,40]{0,1:T(8,128)(2,1)}, u32[]{:S(2)}) copy-start(bf16[100,40]{0,1:T(8,128)(2,1)} %param.10) | copy-start | bytes 24004
  10.8 53.7 %all-to-all-start = ((bf16[25,4,16384]{2,0,1:T(8,128)(2,1)}), bf16[25,4,16384]{2,0,1:T(8,128)(2,1)}, u32[]{:S(2)}, u32[]{:S(2)}) async-start(bf16[25,4,16384]{2,0,1:T(8,128)(2,1)} %copy.24), calls=%async_computation | async-start | bytes 8388608 | tf_op jit(solution)/shard_map/all_to_all | solution.py:152
  72.8 3.8 %copy-start.4 = (s32[1,4096]{1,0:T(1,128)S(1)}, s32[1,4096]{1,0:T(1,128)}, u32[]{:S(2)}) copy-start(s32[1,4096]{1,0:T(1,128)} %lower.1) | copy-start | bytes 49156
  72.8 3.8 %copy-start.5 = (s32[1,4096]{1,0:T(1,128)S(1)}, s32[1,4096]{1,0:T(1,128)}, u32[]{:S(2)}) copy-start(s32[1,4096]{1,0:T(1,128)} %upper.1) | copy-start | bytes 49156
  72.8 6.9 %copy-start.6 = (f32[10]{0:T(128)S(1)}, f32[10]{0:T(128)}, u32[]{:S(2)}) copy-start(f32[10]{0:T(128)} %param.11) | copy-start | bytes 124
  72.8 28.5 %all-to-all-start.1 = ((bf16[4,10,16384]{2,1,0:T(8,128)(2,1)}), bf16[4,10,16384]{2,1,0:T(8,128)(2,1)S(1)}, u32[]{:S(2)}, u32[]{:S(2)}) async-start(bf16[4,10,16384]{2,1,0:T(8,128)(2,1)} %all_to_all.35), calls=%async_computation.1 | async-start | bytes 4194304 | tf_op jit(solution)/shard_map/all_to_all | solution.py:154
  76.6 4.1 %collective-permute-start.2 = (s32[1,8320]{1,0:T(1,128)S(1)}, s32[1,8320]{1,0:T(1,128)S(1)}, u32[]{:S(2)}, u32[]{:S(2)}) collective-permute-start(s32[1,8320]{1,0:T(1,128)S(1)} %reshape_add_fusion), channel_id=1, source_target_pairs={{0,4},{4,8},{8,12},{12,16},{16,20},{20,24},{24,28},{28,32},{32,36}... | collective-permute-start | bytes 99848 | tf_op jit(solution)/shard_map/ppermute | solution.py:147
  104.3 8.0 %copy-start.1 = (f32[65536]{0:T(1024)S(1)}, f32[65536]{0:T(1024)}, u32[]{:S(2)}) copy-start(f32[65536]{0:T(1024)} %param.14) | copy-start | bytes 786436
  104.3 8.0 %copy-start.2 = (f32[65536]{0:T(1024)S(1)}, f32[65536]{0:T(1024)}, u32[]{:S(2)}) copy-start(f32[65536]{0:T(1024)} %param.13) | copy-start | bytes 786436
  104.3 8.0 %copy-start.3 = (f32[65536]{0:T(1024)S(1)}, f32[65536]{0:T(1024)}, u32[]{:S(2)}) copy-start(f32[65536]{0:T(1024)} %param.12) | copy-start | bytes 786436
  104.3 6.7 %collective-permute-start = (bf16[10,4096]{1,0:T(8,128)(2,1)S(1)}, bf16[10,4096]{1,0:T(8,128)(2,1)S(1)}, u32[]{:S(2)}, u32[]{:S(2)}) collective-permute-start(bf16[10,4096]{1,0:T(8,128)(2,1)S(1)} %get-tuple-element.10), channel_id=1, source_target_pairs={{0,124},{4,0},{8,4},{12,8},{16,12},{20,16},{24,20},{28,24},{32,28}... | collective-permute-start | bytes 245768 | tf_op jit(solution)/shard_map/ppermute | solution.py:147
  106.9 5.4 %collective-permute-start.1 = (bf16[10,4096]{1,0:T(8,128)(2,1)S(1)}, bf16[10,4096]{1,0:T(8,128)(2,1)S(1)}, u32[]{:S(2)}, u32[]{:S(2)}) collective-permute-start(bf16[10,4096]{1,0:T(8,128)(2,1)S(1)} %get-tuple-element.9), channel_id=1, source_target_pairs={{0,4},{4,8},{8,12},{12,16},{16,20},{20,24},{24,28},{28,32},{32,36}... | collective-permute-start | bytes 245768 | tf_op jit(solution)/shard_map/ppermute | solution.py:147

commit v2 on v1

--- a/solution.py
+++ b/solution.py
@@ -14,14 +14,13 @@
 LOW = 256
 
 
-def link_plane(part_a, part_b, gather_ref, scatter_ref, count, link_a, link_b):
+def link_plane(part_a, part_b, gather_ref, scatter_ref, link_a, link_b):
     high = PLANE // LOW
     whole = jnp.concatenate(
         [part_a[...].astype(jnp.float32), part_b[...].astype(jnp.float32), jnp.zeros((6, PLANE), jnp.float32)], axis=0
     ).astype(jnp.bfloat16)
     table = jnp.concatenate([whole[:, LOW * h : LOW * (h + 1)] for h in range(high)], axis=0)
     cell = lax.broadcasted_iota(jnp.int32, (LOW, SLOTS), 0)
-    slot = lax.broadcasted_iota(jnp.int32, (1, SLOTS), 1)
 
     def step(t, total):
         at = pl.multiple_of(t * SLOTS, SLOTS)
@@ -33,7 +32,7 @@
         value = jnp.zeros((16, SLOTS), jnp.float32)
         for h in range(high):
             value = value + jnp.where(source_high == h, rows[16 * h : 16 * h + 16], 0.0)
-        target_high = jnp.where(slot + at < count, target >> 8, -1)
+        target_high = target >> 8
         spread = jnp.concatenate(
             [jnp.where(target_high == h, value, 0.0).astype(jnp.bfloat16) for h in range(high)], axis=0
         )
@@ -111,11 +110,11 @@
 
 
 def finish_kernel(
-    ea, eb, above_a, above_b, below_a, below_b, lower, upper, down_lower, down_upper, counts,
+    ea, eb, above_a, above_b, below_a, below_b, lower, upper, down_lower, down_upper,
     mass, damping, stiffness, eigen, eig_ref, res_ref, sums_ref, first_a, first_b, last_a, last_b,
 ):
-    link_plane(below_a, below_b, down_lower, down_upper, counts[1], first_a, first_b)
-    link_plane(above_a, above_b, upper, lower, counts[0], last_a, last_b)
+    link_plane(below_a, below_b, down_lower, down_upper, first_a, first_b)
+    link_plane(above_a, above_b, upper, lower, last_a, last_b)
     residual_all(
         ea, eb, (mass, damping, stiffness), eigen, ((first_a, first_b), (last_a, last_b)), eig_ref, res_ref, sums_ref
     )
@@ -124,7 +123,7 @@
 def finish(*operands):
     rows = operands[0].shape[1]
     vmem = pl.BlockSpec(memory_space=pltpu.VMEM)
-    specs = [vmem] * 10 + [pl.BlockSpec(memory_space=pltpu.SMEM)] + [vmem] * 4
+    specs = [vmem] * 14
     plane = lambda r: pltpu.VMEM((r, PLANE), jnp.float32)
     return pl.pallas_call(
         finish_kernel,
@@ -141,28 +140,197 @@
     )(*operands)
 
 
-def from_behind(value, axis, steps):
-    count = lax.axis_size(axis)
-    pairs = [(source, (source + steps) % count) for source in range(count)]
-    return lax.ppermute(value, axis, pairs)
+MESH = pl.DeviceIdType.MESH
+PIECE = 2048
+CHUNK = 4 * PIECE
+HALF = PIECE // 2
+ORDER = (0, 7, 1, 2, 3, 4, 5, 6)
+AHEAD = 3
+
+
+def exchange_kernel(
+    basis, extra, coefs, lists, ea, eb, above_a, above_b, below_a, below_b, down_lists,
+    ra, rb, sa, sb, own_sem, own_extra_sem, basis_sem, extra_sem, vec_a_sem, vec_b_sem, plane_sem,
+):
+    me, sub = lax.axis_index("vecs"), lax.axis_index("rows")
+    subs = lax.axis_size("rows")
+    following, previous = lax.rem(sub + 1, subs), lax.rem(sub + subs - 1, subs)
+    ahead = [lax.rem(me + d, 4) for d in (1, 2, 3)]
+    behind = [lax.rem(me + 4 - d, 4) for d in (1, 2, 3)]
+    order = (0, 2, 1)
+
+    barrier = pltpu.get_barrier_semaphore()
+    for peer in ahead:
+        pl.semaphore_signal(barrier, inc=1, device_id={"vecs": peer}, device_id_type=MESH)
+    for peer in (following, previous):
+        pl.semaphore_signal(barrier, inc=1, device_id={"rows": peer}, device_id_type=MESH)
+    pl.semaphore_wait(barrier, 5)
+
+    def remote(source, target, sems, at, peer):
+        return pltpu.make_async_remote_copy(
+            src_ref=source, dst_ref=target, send_sem=sems.at[(0, *at)], recv_sem=sems.at[(1, *at)],
+            device_id=peer, device_id_type=MESH,
+        )
+
+    def columns(c, q):
+        return pl.ds(pl.multiple_of(c * CHUNK + q * PIECE, PIECE), PIECE)
+
+    def send_basis(c):
+        for d in order:
+            peer = ahead[d]
+            for g in range(3):
+                remote(
+                    basis.at[pl.ds(8 * g, 8), columns(c, peer)], ra.at[c, g, me], basis_sem, (c, d, g), {"vecs": peer}
+                ).start()
+            remote(extra.at[c, peer], rb.at[c, me], extra_sem, (c, d), {"vecs": peer}).start()
+
+    def own_copies(c):
+        for g in range(3):
+            yield pltpu.make_async_copy(
+                basis.at[pl.ds(8 * g, 8), columns(c, me)], ra.at[c, g, me], own_sem.at[c, g]
+            )
+        yield pltpu.make_async_copy(extra.at[c, me], rb.at[c, me], own_extra_sem.at[c])
+
+    def basis_arrivals(c):
+        for d in order:
+            for g in range(3):
+                block = ra.at[c, g, behind[d]]
+                yield remote(block, block, basis_sem, (c, d, g), {"vecs": ahead[d]})
+            block = rb.at[c, behind[d]]
+            yield remote(block, block, extra_sem, (c, d), {"vecs": ahead[d]})
+
+    def vec_copies(c):
+        for d in order:
+            peer = ahead[d]
+            yield remote(sa.at[c, peer], ea.at[:, columns(c, me)], vec_a_sem, (c, d), {"vecs": peer})
+            yield remote(sb.at[c, peer], eb.at[:, columns(c, me)], vec_b_sem, (c, d), {"vecs": peer})
+
+    def vec_arrivals(c):
+        for d in order:
+            block = ea.at[:, columns(c, behind[d])]
+            yield remote(block, block, vec_a_sem, (c, d), {"vecs": ahead[d]})
+            block = eb.at[:, columns(c, behind[d])]
+            yield remote(block, block, vec_b_sem, (c, d), {"vecs": ahead[d]})
+
+    rows_local = basis.shape[1]
+    plane_copies = {
+        ORDER[0]: (
+            remote(ea.at[:, pl.ds(0, PLANE)], above_a, plane_sem, (0,), {"rows": previous}),
+            remote(eb.at[:, pl.ds(0, PLANE)], above_b, plane_sem, (1,), {"rows": previous}),
+        ),
+        ORDER[1]: (
+            remote(ea.at[:, pl.ds(rows_local - PLANE, PLANE)], below_a, plane_sem, (2,), {"rows": following}),
+            remote(eb.at[:, pl.ds(rows_local - PLANE, PLANE)], below_b, plane_sem, (3,), {"rows": following}),
+        ),
+    }
+    list_copy = remote(lists, down_lists, plane_sem, (4,), {"rows": following})
+
+    for c in ORDER[:AHEAD]:
+        send_basis(c)
+    list_copy.start()
+    for c in ORDER:
+        for copy in own_copies(c):
+            copy.start()
+
+    def product(c):
+        for h in range(2):
+            at = pl.ds(h * HALF, HALF)
+            parts = [ra[c, g, :, :, at].reshape(32, HALF) for g in range(3)]
+            odd = jnp.concatenate(
+                [rb[c, q].astype(jnp.float32) for q in range(4)] + [jnp.zeros((24, HALF), jnp.float32)], axis=0
+            )
+            whole = jnp.concatenate([*parts, odd.astype(jnp.bfloat16)], axis=0)
+            out = jnp.dot(coefs[h], whole, preferred_element_type=jnp.float32)
+            for p in range(4):
+                sa[c, p, :, at] = out[8 * p : 8 * p + 8].astype(jnp.bfloat16)
+                sb[c, p, :, at] = out[32 + 2 * p : 34 + 2 * p].astype(jnp.bfloat16)
+        ea[:, columns(c, me)] = sa[c, me]
+        eb[:, columns(c, me)] = sb[c, me]
+
+    def arrived(c):
+        for copy in vec_arrivals(c):
+            copy.wait_recv()
+        for copy in plane_copies.get(c, ()):
+            copy.start()
+
+    for i, c in enumerate(ORDER):
+        for copy in own_copies(c):
+            copy.wait()
+        for copy in basis_arrivals(c):
+            copy.wait_recv()
+        product(c)
+        for copy in vec_copies(c):
+            copy.start()
+        if i + AHEAD < len(ORDER):
+            send_basis(ORDER[i + AHEAD])
+        if i >= 2:
+            arrived(ORDER[i - 2])
+    arrived(ORDER[-2])
+    arrived(ORDER[-1])
+    for copies in plane_copies.values():
+        for copy in copies:
+            copy.wait()
+    list_copy.wait()
+    for c in ORDER:
+        for copy in basis_arrivals(c):
+            copy.wait_send()
+        for copy in vec_copies(c):
+            copy.wait_send()
+
+
+def exchange(basis, extra, coefs, lists):
+    rows = basis.shape[1]
+    chunks = rows // CHUNK
+    vmem = pl.BlockSpec(memory_space=pltpu.VMEM)
+    hbm = pl.BlockSpec(memory_space=pl.ANY)
+    bf16 = lambda *shape: jax.ShapeDtypeStruct(shape, jnp.bfloat16)
+    dma = pltpu.SemaphoreType.DMA
+    return pl.pallas_call(
+        exchange_kernel,
+        out_shape=(
+            bf16(8, rows), bf16(2, rows), bf16(8, PLANE), bf16(2, PLANE), bf16(8, PLANE), bf16(2, PLANE),
+            jax.ShapeDtypeStruct(lists.shape, jnp.int32),
+        ),
+        in_specs=[hbm, vmem, vmem, vmem],
+        out_specs=(vmem,) * 7,
+        scratch_shapes=[
+            pltpu.VMEM((chunks, 3, 4, 8, PIECE), jnp.bfloat16),
+            pltpu.VMEM((chunks, 4, 2, HALF), jnp.bfloat16),
+            pltpu.VMEM((chunks, 4, 8, PIECE), jnp.bfloat16),
+            pltpu.VMEM((chunks, 4, 2, PIECE), jnp.bfloat16),
+            dma((chunks, 3)), dma((chunks,)), dma((2, chunks, 3, 3)), dma((2, chunks, 3)),
+            dma((2, chunks, 3)), dma((2, chunks, 3)), dma((2, 5)),
+        ],
+        compiler_params=pltpu.CompilerParams(
+            collective_id=0, has_side_effects=True, vmem_limit_bytes=48 * 2**20
+        ),
+        name="exchange",
+    )(basis, extra, coefs, lists)
+
+
+def spread_coefficients(coefficients):
+    by_vec = coefficients.T.reshape(4, 10, 4, 25)
+    ordered = jnp.concatenate([by_vec[:, :8].reshape(32, 4, 25), by_vec[:, 8:].reshape(8, 4, 25)], axis=0)
+    main = ordered[:, :, :24].reshape(40, 4, 3, 8).transpose(0, 2, 1, 3).reshape(40, 96)
+    odd = ordered[:, :, 24]
+    none = jnp.zeros_like(odd)
+    pad = jnp.zeros((40, 24), coefficients.dtype)
+    halves = [jnp.stack([odd, none], axis=2), jnp.stack([none, odd], axis=2)]
+    return jnp.stack([jnp.concatenate([main, half.reshape(40, 8), pad], axis=1) for half in halves])
 
 
 def on_device(basis, coefficients, eigen_values, stiffness, damping, mass, link_count, lower_cells, upper_cells):
     rows_local = basis.shape[1]
-    quarter = lax.all_to_all(basis, "vecs", split_axis=1, concat_axis=0, tiled=True)
-    quarter_vecs = jnp.dot(coefficients.T, quarter, preferred_element_type=jnp.float32).astype(jnp.bfloat16)
-    eigvecs = lax.all_to_all(quarter_vecs, "vecs", split_axis=0, concat_axis=1, tiled=True)
-    lists = jnp.concatenate([lower_cells, upper_cells, jnp.broadcast_to(link_count[:, None], (1, 128))], axis=1)
-    down = from_behind(lists, "rows", 1)
-    slots = lower_cells.shape[1]
-    down_lower, down_upper, down_count = down[:, :slots], down[:, slots : 2 * slots], down[0, 2 * slots :][:1]
-    ea, eb = eigvecs[:8], eigvecs[8:]
-    below = from_behind(eigvecs[:, rows_local - PLANE :], "rows", 1)
-    above = from_behind(eigvecs[:, :PLANE], "rows", -1)
+    extra = basis[24].reshape(rows_local // CHUNK, 4, 2, HALF)
+    used = jnp.arange(lower_cells.shape[1], dtype=jnp.int32)[None, :] < link_count[0]
+    lists = jnp.where(used, jnp.concatenate([lower_cells, upper_cells], axis=0), -1)
+    ea, eb, above_a, above_b, below_a, below_b, down = exchange(
+        basis, extra, spread_coefficients(coefficients), lists
+    )
     wide = lambda a: a.reshape(1, rows_local)
     eig, res, sums = finish(
-        ea, eb, above[:8], above[8:], below[:8], below[8:], lower_cells, upper_cells, down_lower, down_upper,
-        jnp.concatenate([link_count, down_count]), wide(mass), wide(damping), wide(stiffness), eigen_values[:, None],
+        ea, eb, above_a, above_b, below_a, below_b, lists[:1], lists[1:], down[:1], down[1:],
+        wide(mass), wide(damping), wide(stiffness), eigen_values[:, None],
     )
     local = jnp.sum(sums, axis=2).reshape(1, 20)
     devices = lax.axis_size("rows")

time: 145 us -> 99.1 us (0.68)
  waiting for transfers between devices: 71.8 us -> 0 us
  Pallas kernels: 15.3 us -> 69 us
  starting transfers between devices: 15.9 us -> 0 us
  local copies, waits for them, and re-layouts: 20.5 us -> 6.5 us
  blocking collectives: 16.6 us -> 20.1 us
  matrix products: 1.89 us -> 0 us
    all_to_all x2 -> x0, waiting for transfers between devices: 68.2 us -> none  [the longest x1 48.1 us: on_device(): lax.all_to_all(basis, 'vecs', split_axis=1, concat_axis=0, tiled=True)]
    pallas_call x0 -> x1, Pallas kernels: none -> 54.3 us  [exchange(): pl.pallas_call(exchange_kernel, out_shape=(bf16(8, rows), bf16(2, rows),...]
    all_to_all x5 -> x0, local copies, waits for them, and re-layouts: 17.6 us -> none  [the longest x3 13.5 us: on_device(): lax.all_to_all(basis, 'vecs', split_axis=1, concat_axis=0, tiled=True)]
    all_to_all x2 -> x0, starting transfers between devices: 8.58 us -> none  [the longest x1 4.84 us: on_device(): lax.all_to_all(basis, 'vecs', split_axis=1, concat_axis=0, tiled=True)]
    ppermute x3 -> x0, starting transfers between devices: 7.36 us -> none  [from_behind(): return lax.ppermute(value, axis, pairs)]
    ppermute x3 -> x0, waiting for transfers between devices: 3.59 us -> none  [from_behind(): return lax.ppermute(value, axis, pairs)]
    all_to_all x1, blocking collectives: 16.6 us -> 20.1 us  [on_device(): lax.all_to_all(jnp.broadcast_to(local[None], (devices, 1, 20)), 'rows', 0...]
    dot_general x1 -> x0, matrix products: 1.89 us -> none  [on_device(): jnp.dot(coefficients.T, quarter, preferred_element_type=jnp.float32)]
  transfers between devices with their start and end apart: 5 -> 0, of which waited for: 5 -> 0; matrix products, arithmetic and copies ran while one was open for 1% -> 0% of each run, Pallas kernels for 0% -> 0%
where the time goes in v2:
time: 99.1 us; the launch traced here: 98.7 us
  Pallas kernels  69 us (70%)
  blocking collectives  20.1 us (20%)
  local copies, waits for them, and re-layouts  6.5 us (7%)
  other arithmetic  1.7 us (2%)
  between operations  1.45 us (1%)
    pallas_call x1, Pallas kernels, exchange(): pl.pallas_call(exchange_kernel, out_shape=(bf16(8, rows), bf16(2, rows),...  54.3 us
    all_to_all x1, blocking collectives, on_device(): lax.all_to_all(jnp.broadcast_to(local[None], (devices, 1, 20)), 'rows', 0...  20.1 us
    pallas_call x1, Pallas kernels, finish(): pl.pallas_call(finish_kernel, out_shape=(jax.ShapeDtypeStruct((10, rows),...  14.7 us
    unnamed x11, local copies, waits for them, and re-layouts  2.32 us

profile of v2, /device:TPU:1, one launch (start us, length us, event | category | flops | bytes accessed | tf_op | source)
XLA Modules:
  0.0 98.7 jit_solution(13457831259082849107)
XLA Ops:
  0.6 0.0 copy-start.1
  0.6 0.0 copy-start.2
  0.7 0.0 copy-start.3
  0.7 0.9 reshape.55
  1.6 0.1 pad_maximum_fusion
  2.4 0.7 copy.66.eigen
  3.1 0.1 copy.71
  3.2 0.1 copy.58
  3.3 0.1 copy.61
  3.4 0.1 copy.65
  3.5 0.1 copy.62
  3.6 1.9 %slice_reduce_fusion = bf16[65536]{0:T(1024)(128)(2,1)S(1)} fusion(bf16[25,65536]{1,0:T(8,128)(2,1)} %basis.1), kind=kLoop, calls=%fused_computation | loop fusion | bytes 262144 | tf_op jit(solution)/shard_map/slice | solution.py:324
  5.6 0.1 pad.11.clone
  5.7 0.1 maximum_bitcast_fusion
  5.7 0.8 add_select_fusion.lists
  6.5 0.0 copy-start
  6.5 2.2 %copy-done = bf16[25,65536]{1,0:T(8,128)(2,1)S(1)} copy-done((bf16[25,65536]{1,0:T(8,128)(2,1)S(1)}, bf16[25,65536]{1,0:T(8,128)(2,1)}, u32[]{:S(2)}) %copy-start) | copy-done | bytes 3276824
  8.7 54.3 %exchange.1 = (bf16[8,65536]{1,0:T(8,128)(2,1)S(1)}, bf16[2,65536]{1,0:T(2,128)(2,1)S(1)}, bf16[8,4096]{1,0:T(8,128)(2,1)S(1)}, bf16[2,4096]{1,0:T(2,128)(2,1)S(...) custom-call(bf16[25,65536]{1,0:T(8,128)(2,1)S(1)} %copy-done, ...), custom_call_target="tpu_custom_call" | custom-call | tf_op jit(solution)/shard_map/exchange/pallas_call | solution.py:288
  63.0 0.1 fusion
  63.0 0.0 copy-done.1
  63.1 0.0 copy-done.2
  63.1 0.0 copy-done.3
  63.1 14.7 %finish.1 = (bf16[10,65536]{1,0:T(8,128)(2,1)}, bf16[10,65536]{1,0:T(8,128)(2,1)}, f32[2,10,128]{2,1,0:T(8,128)S(1)}) custom-call(bf16[8,65536]{1,0:T(8,128)(2,1)S(1)} %get-tuple-element.13.ea, bf16[2,65536]{1,0:T(2,128)(2,1)S(1)} %get-tuple-element.14.eb, bf16[8,4096]{1,0:T(8,128)(2,1)S(1)} %get-tuple-element.15.above_a, ...), custom_call_target="tpu_custom_call" | custom-call | tf_op jit(solution)/shard_map/finish/pallas_call | solution.py:128
  77.8 0.1 reduce_sum.20
  77.9 0.1 broadcast_in_dim.30
  78.0 20.1 %all_to_all.5 = f32[32,1,20]{2,1,0:T(1,128)S(1)} all-to-all(f32[32,1,20]{2,1,0:T(1,128)S(1)} %broadcast_in_dim.31), channel_id=1, replica_groups=mesh['rows'=32,'vecs'=4] {'rows'}, dimensions={0} | all-to-all | bytes 5120 | tf_op jit(solution)/shard_map/all_to_all | solution.py:337
  98.0 0.1 reduce_sum.21
  98.1 0.6 multiply_bitcast_fusion
  (12 shorter events, 0.1 us)
Async XLA Ops:
  0.6 62.4 %copy-start.1 = (f32[65536]{0:T(1024)S(1)}, f32[65536]{0:T(1024)}, u32[]{:S(2)}) copy-start(f32[65536]{0:T(1024)} %param.14) | copy-start | bytes 786436
  0.6 62.4 %copy-start.2 = (f32[65536]{0:T(1024)S(1)}, f32[65536]{0:T(1024)}, u32[]{:S(2)}) copy-start(f32[65536]{0:T(1024)} %param.13) | copy-start | bytes 786436
  0.7 62.4 %copy-start.3 = (f32[65536]{0:T(1024)S(1)}, f32[65536]{0:T(1024)}, u32[]{:S(2)}) copy-start(f32[65536]{0:T(1024)} %param.12) | copy-start | bytes 786436
  6.5 2.2 %copy-start = (bf16[25,65536]{1,0:T(8,128)(2,1)S(1)}, bf16[25,65536]{1,0:T(8,128)(2,1)}, u32[]{:S(2)}) copy-start(bf16[25,65536]{1,0:T(8,128)(2,1)} %basis.1) | copy-start | bytes 9830404

commit v3 on v2

v3 whole, which is shorter than its diff:
```python
import functools

import jax
import jax.numpy as jnp
from jax import lax
from jax.experimental import pallas as pl
from jax.experimental.pallas import tpu as pltpu
from jax.sharding import PartitionSpec as P

WID = 64
PLANE = WID * WID
SPAN = 1024
SLOTS = 512
LOW = 256


def link_plane(part_a, part_b, lists, gather, scatter, link_a, link_b):
    high = PLANE // LOW
    whole = jnp.concatenate(
        [part_a[...].astype(jnp.float32), part_b[...].astype(jnp.float32), jnp.zeros((6, PLANE), jnp.float32)], axis=0
    ).astype(jnp.bfloat16)
    table = jnp.concatenate([whole[:, LOW * h : LOW * (h + 1)] for h in range(high)], axis=0)
    cell = lax.broadcasted_iota(jnp.int32, (LOW, SLOTS), 0)

    def step(t, total):
        at = pl.multiple_of(t * SLOTS, SLOTS)
        source = lists[gather : gather + 1, pl.ds(at, SLOTS)]
        target = lists[scatter : scatter + 1, pl.ds(at, SLOTS)]
        pick = jnp.where(cell == (source & (LOW - 1)), 1.0, 0.0).astype(jnp.bfloat16)
        rows = jnp.dot(table, pick, preferred_element_type=jnp.float32)
        source_high = source >> 8
        value = jnp.zeros((16, SLOTS), jnp.float32)
        for h in range(high):
            value = value + jnp.where(source_high == h, rows[16 * h : 16 * h + 16], 0.0)
        target_high = target >> 8
        spread = jnp.concatenate(
            [jnp.where(target_high == h, value, 0.0).astype(jnp.bfloat16) for h in range(high)], axis=0
        )
        place = jnp.where(cell == (target & (LOW - 1)), 1.0, 0.0).astype(jnp.bfloat16)
        return total + lax.dot_general(
            spread, place, (((1,), (1,)), ((), ())), preferred_element_type=jnp.float32
        )

    total = lax.fori_loop(0, PLANE // SLOTS, step, jnp.zeros((16 * high, LOW), jnp.float32))
    for h in range(high):
        link_a[:, LOW * h : LOW * (h + 1)] = total[16 * h : 16 * h + 8]
        link_b[:, LOW * h : LOW * (h + 1)] = total[16 * h + 8 : 16 * h + 10]


def residual_spans(vecs, outs, diag_refs, eigen, first, planes, links, sums):
    eig_ref, res_ref = outs
    depth = eig_ref.shape[1] // PLANE
    spans = PLANE // SPAN
    column = lax.broadcasted_iota(jnp.int32, (1, SPAN), 1) & (WID - 1)
    groups = ((vecs[0], slice(0, 8)), (vecs[1], slice(8, 10)))
    factors = []
    for _, part in groups:
        lam = eigen[part]
        factors.append((lam, lam * lam, lam * lam * 0.1 + lam * 0.3 + 1.0))

    def step(i, totals):
        c = i % spans
        base = pl.multiple_of(first * PLANE + i * SPAN, SPAN)
        here = pl.ds(base, SPAN)
        before = pl.ds(pl.multiple_of(jnp.where(c > 0, base - 128, base), 128), 128)
        after = pl.ds(pl.multiple_of(jnp.where(c < spans - 1, base + SPAN, base), 128), 128)
        mass, damping, stiffness = (r[:, here] for r in diag_refs)
        done = []
        for k, (ref, part) in enumerate(groups):
            lam, square, coupling = factors[k]
            raw = ref[:, here]
            value = raw.astype(jnp.float32)
            left = jnp.where(c > 0, ref[:, before].astype(jnp.float32), 0.0)
            right = jnp.where(c < spans - 1, ref[:, after].astype(jnp.float32), 0.0)
            wide = jnp.concatenate([left, value, right], axis=1)
            span = SPAN + 256
            total = pltpu.roll(wide, WID, 1)[:, 128 : 128 + SPAN] + pltpu.roll(wide, span - WID, 1)[:, 128 : 128 + SPAN]
            total = total + jnp.where(column > 0, pltpu.roll(value, 1, 1), 0.0)
            total = total + jnp.where(column < WID - 1, pltpu.roll(value, SPAN - 1, 1), 0.0)
            if not (links is not None and first == 0):
                total = total + ref[:, pl.ds(pl.multiple_of(base - PLANE, SPAN), SPAN)].astype(jnp.float32)
            if not (links is not None and first == depth - 1):
                total = total + ref[:, pl.ds(pl.multiple_of(base + PLANE, SPAN), SPAN)].astype(jnp.float32)
            if links is not None:
                total = total + links[k][:, pl.ds(pl.multiple_of(i * SPAN, SPAN), SPAN)]
            residual = (square * mass + lam * damping + stiffness) * value - coupling * total
            eig_ref[part, here] = raw
            res_ref[part, here] = residual.astype(jnp.bfloat16)
            vector_sq, residual_sq = totals[2 * k], totals[2 * k + 1]
            for t in range(SPAN // 128):
                lanes = slice(128 * t, 128 * (t + 1))
                vector_sq = vector_sq + value[:, lanes] * value[:, lanes]
                residual_sq = residual_sq + residual[:, lanes] * residual[:, lanes]
            done += [vector_sq, residual_sq]
        return tuple(done)

    totals = lax.fori_loop(0, planes * spans, step, tuple(ref[...] for ref in sums))
    for ref, total in zip(sums, totals):
        ref[...] = total


def column_of(row):
    n = row.shape[1]
    same = lax.broadcasted_iota(jnp.int32, (n, n), 0) == lax.broadcasted_iota(jnp.int32, (n, n), 1)
    return jnp.sum(jnp.where(same, row, 0.0), axis=1, keepdims=True)


def spread_coefficients(coefficients, coefs):
    out = lax.broadcasted_iota(jnp.int32, (40, 40), 0)
    vec = lax.broadcasted_iota(jnp.int32, (40, 40), 1)
    rest = out - 32
    wanted = jnp.where(out < 32, 10 * (out >> 3) + (out & 7), 10 * (rest >> 1) + 8 + (rest & 1))
    rows = jnp.where(vec == wanted, 1.0, 0.0).astype(jnp.bfloat16)
    ordered = jnp.dot(rows, coefficients[...], preferred_element_type=jnp.float32).astype(jnp.bfloat16)
    rank = lax.broadcasted_iota(jnp.int32, (100, 128), 0)
    at = lax.broadcasted_iota(jnp.int32, (100, 128), 1)
    odd = at - 96
    for h in range(2):
        main = 25 * ((at >> 3) & 3) + 8 * (at >> 5) + (at & 7)
        other = jnp.where((odd < 8) & ((odd & 1) == h), 25 * (odd >> 1) + 24, -1)
        pick = jnp.where(rank == jnp.where(at < 96, main, other), 1.0, 0.0).astype(jnp.bfloat16)
        coefs[h] = jnp.dot(ordered, pick, preferred_element_type=jnp.float32).astype(jnp.bfloat16)


MESH = pl.DeviceIdType.MESH
PIECE = 2048
CHUNK = 4 * PIECE
HALF = PIECE // 2
ORDER = (0, 7, 1, 2, 3, 4, 5, 6)
AHEAD = 3


def whole_kernel(
    basis, coefficients, lists, mass, damping, stiffness, eigen_row, eig_ref, res_ref, norm_ref,
    odd_rows, extra, coefs, ea, eb, above_a, above_b, below_a, below_b, down_lists, ra, rb, sa, sb,
    first_a, first_b, last_a, last_b, square_a, residual_a, square_b, residual_b, squares,
    own_sem, odd_sem, basis_sem, extra_sem, vec_a_sem, vec_b_sem, plane_sem, square_sem,
):
    me, sub = lax.axis_index("vecs"), lax.axis_index("rows")
    subs = lax.axis_size("rows")
    following, previous = lax.rem(sub + 1, subs), lax.rem(sub + subs - 1, subs)
    ahead = [lax.rem(me + d, 4) for d in (1, 2, 3)]
    behind = [lax.rem(me + 4 - d, 4) for d in (1, 2, 3)]
    order = (0, 2, 1)

    barrier = pltpu.get_barrier_semaphore()
    for peer in ahead:
        pl.semaphore_signal(barrier, inc=1, device_id={"vecs": peer}, device_id_type=MESH)

    @pl.loop(1, subs)
    def _(d):
        pl.semaphore_signal(barrier, inc=1, device_id={"rows": lax.rem(sub + d, subs)}, device_id_type=MESH)

    def remote(source, target, sems, at, peer):
        return pltpu.make_async_remote_copy(
            src_ref=source, dst_ref=target, send_sem=sems.at[(0, *at)], recv_sem=sems.at[(1, *at)],
            device_id=peer, device_id_type=MESH,
        )

    def columns(c, q):
        return pl.ds(pl.multiple_of(c * CHUNK + q * PIECE, PIECE), PIECE)

    def send_basis(c):
        for d in order:
            peer = ahead[d]
            for g in range(3):
                remote(
                    basis.at[pl.ds(8 * g, 8), columns(c, peer)], ra.at[c, g, me], basis_sem, (c, d, g), {"vecs": peer}
                ).start()

    def send_extra(c):
        for d in order:
            peer = ahead[d]
            remote(extra.at[c, peer], rb.at[c, me], extra_sem, (c, d), {"vecs": peer}).start()

    def own_copies(c):
        for g in range(3):
            yield pltpu.make_async_copy(
                basis.at[pl.ds(8 * g, 8), columns(c, me)], ra.at[c, g, me], own_sem.at[c, g]
            )

    def basis_arrivals(c):
        for d in order:
            for g in range(3):
                block = ra.at[c, g, behind[d]]
                yield remote(block, block, basis_sem, (c, d, g), {"vecs": ahead[d]})
            block = rb.at[c, behind[d]]
            yield remote(block, block, extra_sem, (c, d), {"vecs": ahead[d]})

    def vec_copies(c):
        for d in order:
            peer = ahead[d]
            yield remote(sa.at[c, peer], ea.at[:, columns(c, me)], vec_a_sem, (c, d), {"vecs": peer})
            yield remote(sb.at[c, peer], eb.at[:, columns(c, me)], vec_b_sem, (c, d), {"vecs": peer})

    def vec_arrivals(c):
        for d in order:
            block = ea.at[:, columns(c, behind[d])]
            yield remote(block, block, vec_a_sem, (c, d), {"vecs": ahead[d]})
            block = eb.at[:, columns(c, behind[d])]
            yield remote(block, block, vec_b_sem, (c, d), {"vecs": ahead[d]})

    rows_local = basis.shape[1]
    plane_copies = {
        ORDER[0]: (
            remote(ea.at[:, pl.ds(0, PLANE)], above_a, plane_sem, (0,), {"rows": previous}),
            remote(eb.at[:, pl.ds(0, PLANE)], above_b, plane_sem, (1,), {"rows": previous}),
        ),
        ORDER[1]: (
            remote(ea.at[:, pl.ds(rows_local - PLANE, PLANE)], below_a, plane_sem, (2,), {"rows": following}),
            remote(eb.at[:, pl.ds(rows_local - PLANE, PLANE)], below_b, plane_sem, (3,), {"rows": following}),
        ),
    }
    list_copy = remote(lists, down_lists, plane_sem, (4,), {"rows": following})

    odd_copy = pltpu.make_async_copy(basis.at[pl.ds(24, 1), :], odd_rows, odd_sem)
    odd_copy.start()
    for c in ORDER:
        for copy in own_copies(c):
            copy.start()
    spread_coefficients(coefficients, coefs)
    pl.semaphore_wait(barrier, subs + 2)
    for c in ORDER[:AHEAD]:
        send_basis(c)
    list_copy.start()
    odd_copy.wait()
    for c in ORDER:
        for q in range(4):
            at = c * CHUNK + q * PIECE
            pair = [odd_rows[0:1, at + h * HALF : at + (h + 1) * HALF].astype(jnp.float32) for h in range(2)]
            extra[c, q] = jnp.concatenate(pair, axis=0).astype(jnp.bfloat16)
    for c in ORDER:
        rb[c, me] = extra[c, me]
    for c in ORDER[:AHEAD]:
        send_extra(c)
    sums = (square_a, residual_a, square_b, residual_b)
    for ref in sums:
        ref[...] = jnp.zeros_like(ref)
    eigen = column_of(eigen_row[...])
    diag_refs = (mass, damping, stiffness)

    def planes_done(first, planes, links=None):
        residual_spans((ea, eb), (eig_ref, res_ref), diag_refs, eigen, first, planes, links, sums)

    def product(c):
        for h in range(2):
            at = pl.ds(h * HALF, HALF)
            parts = [ra[c, g, :, :, at].reshape(32, HALF) for g in range(3)]
            odd = jnp.concatenate(
                [rb[c, q].astype(jnp.float32) for q in range(4)] + [jnp.zeros((24, HALF), jnp.float32)], axis=0
            )
            whole = jnp.concatenate([*parts, odd.astype(jnp.bfloat16)], axis=0)
            out = jnp.dot(coefs[h], whole, preferred_element_type=jnp.float32)
            for p in range(4):
                sa[c, p, :, at] = out[8 * p : 8 * p + 8].astype(jnp.bfloat16)
                sb[c, p, :, at] = out[32 + 2 * p : 34 + 2 * p].astype(jnp.bfloat16)
        ea[:, columns(c, me)] = sa[c, me]
        eb[:, columns(c, me)] = sb[c, me]

    def arrived(c):
        for copy in vec_arrivals(c):
            copy.wait_recv()
        for copy in plane_copies.get(c, ()):
            copy.start()

    def first_links():
        for copy in plane_copies[ORDER[1]]:
            copy.wait_recv()
        list_copy.wait_recv()
        link_plane(below_a, below_b, down_lists, 0, 1, first_a, first_b)

    def last_links():
        for copy in plane_copies[ORDER[0]]:
            copy.wait_recv()
        link_plane(above_a, above_b, lists, 1, 0, last_a, last_b)

    def outer_planes():
        planes_done(0, 1, (first_a, first_b))
        planes_done(rows_local // PLANE - 1, 1, (last_a, last_b))

    later = {5: first_links, 6: last_links, 7: outer_planes}
    for i, c in enumerate(ORDER):
        for copy in own_copies(c):
            copy.wait()
        for copy in basis_arrivals(c):
            copy.wait_recv()
        product(c)
        for copy in vec_copies(c):
            copy.start()
        if i + AHEAD < len(ORDER):
            send_basis(ORDER[i + AHEAD])
            send_extra(ORDER[i + AHEAD])
        if i >= 2:
            arrived(ORDER[i - 2])
            if i >= 4:
                planes_done(2 * ORDER[i - 2] - 1, 2)
        if i in later:
            later[i]()
    arrived(ORDER[-2])
    planes_done(2 * ORDER[-2] - 1, 2)
    arrived(ORDER[-1])
    planes_done(2 * ORDER[-1] - 1, 4)

    lane = lax.broadcasted_iota(jnp.int32, (1, 128), 1)
    message = jnp.zeros((1, 128), jnp.float32)
    for ref, start in ((square_a, 0), (square_b, 8), (residual_a, 16), (residual_b, 24)):
        column = jnp.sum(ref[...], axis=1, keepdims=True)
        row = lax.broadcasted_iota(jnp.int32, (ref.shape[0], 128), 0) + start
        message = message + jnp.sum(jnp.where(row == lane, column, 0.0), axis=0, keepdims=True)
    squares[sub] = message

    def square_copy(d):
        return remote(squares.at[sub], squares.at[sub], square_sem, (d,), {"rows": lax.rem(sub + d, subs)})

    @pl.loop(1, subs)
    def _(d):
        square_copy(d).start()

    for copies in plane_copies.values():
        for copy in copies:
            copy.wait_send()
    list_copy.wait_send()
    for c in ORDER:
        for copy in basis_arrivals(c):
            copy.wait_send()
        for copy in vec_copies(c):
            copy.wait_send()

    @pl.loop(1, subs)
    def _(d):
        block = squares.at[lax.rem(sub + subs - d, subs)]
        remote(block, block, square_sem, (d,), {"rows": lax.rem(sub + d, subs)}).wait_recv()

    @pl.loop(1, subs)
    def _(d):
        square_copy(d).wait_send()

    total = jnp.sum(squares[...], axis=0)
    norms = jnp.sqrt(pltpu.roll(total, 112, 1)) / jnp.sqrt(total + 1.0)
    norm_ref[...] = norms[:, :10]


def whole(basis, coefficients, lists, mass, damping, stiffness, eigen_row):
    rows = basis.shape[1]
    chunks = rows // CHUNK
    subs = lax.axis_size("rows")
    vmem = pl.BlockSpec(memory_space=pltpu.VMEM)
    f32 = lambda *shape: pltpu.VMEM(shape, jnp.float32)
    bf16 = lambda *shape: pltpu.VMEM(shape, jnp.bfloat16)
    dma = pltpu.SemaphoreType.DMA
    return pl.pallas_call(
        whole_kernel,
        out_shape=(
            jax.ShapeDtypeStruct((10, rows), jnp.bfloat16),
            jax.ShapeDtypeStruct((10, rows), jnp.bfloat16),
            jax.ShapeDtypeStruct((1, 10), jnp.float32),
        ),
        in_specs=[pl.BlockSpec(memory_space=pltpu.HBM)] + [vmem] * 6,
        out_specs=(vmem,) * 3,
        scratch_shapes=[
            bf16(1, rows), bf16(chunks, 4, 2, HALF), bf16(2, 40, 128), bf16(8, rows), bf16(2, rows),
            bf16(8, PLANE), bf16(2, PLANE), bf16(8, PLANE), bf16(2, PLANE), pltpu.VMEM(lists.shape, jnp.int32),
            bf16(chunks, 3, 4, 8, PIECE), bf16(chunks, 4, 2, HALF), bf16(chunks, 4, 8, PIECE), bf16(chunks, 4, 2, PIECE),
            f32(8, PLANE), f32(2, PLANE), f32(8, PLANE), f32(2, PLANE),
            f32(8, 128), f32(8, 128), f32(2, 128), f32(2, 128), f32(subs, 1, 128),
            dma((chunks, 3)), dma(()), dma((2, chunks, 3, 3)), dma((2, chunks, 3)),
            dma((2, chunks, 3)), dma((2, chunks, 3)), dma((2, 5)), dma((2, subs)),
        ],
        compiler_params=pltpu.CompilerParams(
            collective_id=0, has_side_effects=True, vmem_limit_bytes=48 * 2**20
        ),
        name="whole",
    )(basis, coefficients, lists, mass, damping, stiffness, eigen_row)


def on_device(basis, coefficients, eigen_values, stiffness, damping, mass, link_count, lower_cells, upper_cells):
    rows_local = basis.shape[1]
    used = jnp.arange(lower_cells.shape[1], dtype=jnp.int32)[None, :] < link_count[0]
    lists = jnp.where(used, jnp.concatenate([lower_cells, upper_cells], axis=0), -1)
    wide = lambda a: a.reshape(1, rows_local)
    eig, res, norms = whole(
        basis, coefficients.T, lists, wide(mass), wide(damping), wide(stiffness), eigen_values[None, :]
    )
    return eig, res, norms.reshape(10)


def solution(mesh):
    placed = (
        P("vecs", "rows"), P(), P("vecs"), P("rows"), P("rows"), P("rows"), P("rows"), P("rows", None), P("rows", None),
    )
    return jax.shard_map(
        on_device,
        mesh=mesh,
        in_specs=placed,
        out_specs=(P("vecs", "rows"), P("vecs", "rows"), P("vecs")),
        check_vma=False,
    )
```

time: 99.1 us -> 83.7 us (0.84)
  blocking collectives: 20.1 us -> 0 us
  Pallas kernels: 69 us -> 73.9 us
    all_to_all x1 -> x0, blocking collectives: 20.1 us -> none  [on_device(): lax.all_to_all(jnp.broadcast_to(local[None], (devices, 1, 20)), 'rows', 0...]
    unnamed x11 -> x13, local copies, waits for them, and re-layouts: 2.32 us -> 7.35 us
    pallas_call x2 -> x1, Pallas kernels: 69 us -> 73.9 us  [whole(): pl.pallas_call(whole_kernel, out_shape=(jax.ShapeDtypeStruct((10, rows),...]
    slice x5 -> x0, local copies, waits for them, and re-layouts: 2.07 us -> none  [the longest x1 1.91 us: on_device(): extra = basis[24].reshape(rows_local // CHUNK, 4, 2, HALF)]
    reshape x4 -> x0, local copies, waits for them, and re-layouts: 1.11 us -> none  [the longest x1 0.85 us: spread_coefficients(): by_vec = coefficients.T.reshape(4, 10, 4, 25)]
where the time goes in v3:
time: 83.7 us; the launch traced here: 83.3 us
  Pallas kernels  73.9 us (88%)
  local copies, waits for them, and re-layouts  7.35 us (9%)
  between operations  1.31 us (2%)
    pallas_call x1, Pallas kernels, whole(): pl.pallas_call(whole_kernel, out_shape=(jax.ShapeDtypeStruct((10, rows),...  73.9 us
    unnamed x13, local copies, waits for them, and re-layouts  7.35 us

profile of v3, /device:TPU:1, one launch (start us, length us, event | category | flops | bytes accessed | tf_op | source)
XLA Modules:
  0.0 83.3 jit_solution(15065819098083977999)
XLA Ops:
  1.3 0.8 add_select_fusion.lists
  2.1 0.0 copy-start
  2.1 0.9 %copy-done = f32[65536]{0:T(1024)S(1)} copy-done((f32[65536]{0:T(1024)S(1)}, f32[65536]{0:T(1024)}, u32[]{:S(2)}) %copy-start) | copy-done | bytes 262168
  3.0 0.0 copy-start.1
  3.0 0.9 %copy-done.1 = f32[65536]{0:T(1024)S(1)} copy-done((f32[65536]{0:T(1024)S(1)}, f32[65536]{0:T(1024)}, u32[]{:S(2)}) %copy-start.1) | copy-done | bytes 262168
  4.0 0.0 copy-start.2
  4.0 0.9 %copy-done.2 = f32[65536]{0:T(1024)S(1)} copy-done((f32[65536]{0:T(1024)S(1)}, f32[65536]{0:T(1024)}, u32[]{:S(2)}) %copy-start.2) | copy-done | bytes 262168
  4.9 0.0 copy-start.3
  4.9 0.7 copy-done.3
  5.6 0.0 copy-start.4
  5.6 0.7 copy-done.4
  6.3 73.9 %whole.1 = (bf16[10,65536]{1,0:T(8,128)(2,1)S(1)}, bf16[10,65536]{1,0:T(8,128)(2,1)S(1)}, f32[1,10]{1,0:T(1,128)S(1)}) custom-call(bf16[25,65536]{1,0:T(8,128)(2,1)} %basis.1, bf16[40,100]{1,0:T(8,128)(2,1)S(1)} %bitcast.11, s32[2,4096]{1,0:T(2,128)S(1)} %add_select_fusion.lists, f32[1,65536]{1,0:T(1,128)S(1)} %bitcast.8, f32[1,65536]{1,0:T(1,128)S(1)} %bitcast.9, ...), custom_call_target="tpu_custom_call" | custom-call | tf_op jit(solution)/shard_map/whole/pallas_call | solution.py:351
  80.2 1.3 %copy.16 = bf16[10,65536]{1,0:T(8,128)(2,1)} copy(bf16[10,65536]{1,0:T(8,128)(2,1)S(1)} %get-tuple-element.12) | data formatting | bytes 2621440
  81.5 1.3 %copy.17 = bf16[10,65536]{1,0:T(8,128)(2,1)} copy(bf16[10,65536]{1,0:T(8,128)(2,1)S(1)} %get-tuple-element.13) | data formatting | bytes 2621440
  82.8 0.5 copy.18
  (1 shorter events, 0.0 us)
Async XLA Ops:
  2.1 1.0 %copy-start = (f32[65536]{0:T(1024)S(1)}, f32[65536]{0:T(1024)}, u32[]{:S(2)}) copy-start(f32[65536]{0:T(1024)} %param.14) | copy-start | bytes 786436
  3.0 0.9 %copy-start.1 = (f32[65536]{0:T(1024)S(1)}, f32[65536]{0:T(1024)}, u32[]{:S(2)}) copy-start(f32[65536]{0:T(1024)} %param.13) | copy-start | bytes 786436
  4.0 0.9 %copy-start.2 = (f32[65536]{0:T(1024)S(1)}, f32[65536]{0:T(1024)}, u32[]{:S(2)}) copy-start(f32[65536]{0:T(1024)} %param.12) | copy-start | bytes 786436
  4.9 0.7 copy-start.3
  5.6 0.7 copy-start.4

commit v4 on v3

--- a/solution.py
+++ b/solution.py
@@ -131,10 +131,11 @@
 
 
 def whole_kernel(
-    basis, coefficients, lists, mass, damping, stiffness, eigen_row, eig_ref, res_ref, norm_ref,
+    count, basis, coefficients_in, lower_in, upper_in, mass_in, damping_in, stiffness_in, eigen_in,
+    eig_out, res_out, norm_ref, eig_ref, res_ref, coefficients, lower, upper, mass, damping, stiffness, eigen_row, lists,
     odd_rows, extra, coefs, ea, eb, above_a, above_b, below_a, below_b, down_lists, ra, rb, sa, sb,
     first_a, first_b, last_a, last_b, square_a, residual_a, square_b, residual_b, squares,
-    own_sem, odd_sem, basis_sem, extra_sem, vec_a_sem, vec_b_sem, plane_sem, square_sem,
+    output_sem, input_sem, own_sem, odd_sem, basis_sem, extra_sem, vec_a_sem, vec_b_sem, plane_sem, square_sem,
 ):
     me, sub = lax.axis_index("vecs"), lax.axis_index("rows")
     subs = lax.axis_size("rows")
@@ -213,16 +214,30 @@
     }
     list_copy = remote(lists, down_lists, plane_sem, (4,), {"rows": following})
 
+    inputs = [
+        pltpu.make_async_copy(source, target, input_sem.at[i])
+        for i, (source, target) in enumerate((
+            (coefficients_in, coefficients), (lower_in, lower), (upper_in, upper), (eigen_in, eigen_row),
+            (mass_in, mass), (damping_in, damping), (stiffness_in, stiffness),
+        ))
+    ]
+    inputs[0].start()
     odd_copy = pltpu.make_async_copy(basis.at[pl.ds(24, 1), :], odd_rows, odd_sem)
     odd_copy.start()
     for c in ORDER:
         for copy in own_copies(c):
             copy.start()
+    for copy in inputs[1:]:
+        copy.start()
+    for copy in inputs[:4]:
+        copy.wait()
     spread_coefficients(coefficients, coefs)
+    used = lax.broadcasted_iota(jnp.int32, (1, PLANE), 1) < count[0]
+    lists[0:1, :] = jnp.where(used, lower[...], -1)
+    lists[1:2, :] = jnp.where(used, upper[...], -1)
     pl.semaphore_wait(barrier, subs + 2)
     for c in ORDER[:AHEAD]:
         send_basis(c)
-    list_copy.start()
     odd_copy.wait()
     for c in ORDER:
         for q in range(4):
@@ -233,14 +248,24 @@
         rb[c, me] = extra[c, me]
     for c in ORDER[:AHEAD]:
         send_extra(c)
+    list_copy.start()
     sums = (square_a, residual_a, square_b, residual_b)
     for ref in sums:
         ref[...] = jnp.zeros_like(ref)
     eigen = column_of(eigen_row[...])
     diag_refs = (mass, damping, stiffness)
+    for copy in inputs[4:]:
+        copy.wait()
+
+    output_copies = []
 
     def planes_done(first, planes, links=None):
         residual_spans((ea, eb), (eig_ref, res_ref), diag_refs, eigen, first, planes, links, sums)
+        at = pl.ds(first * PLANE, planes * PLANE)
+        for k, (held, out) in enumerate(((eig_ref, eig_out), (res_ref, res_out))):
+            copy = pltpu.make_async_copy(held.at[:, at], out.at[:, at], output_sem.at[k, first])
+            copy.start()
+            output_copies.append(copy)
 
     def product(c):
         for h in range(2):
@@ -335,12 +360,15 @@
     def _(d):
         square_copy(d).wait_send()
 
+    for copy in output_copies:
+        copy.wait()
     total = jnp.sum(squares[...], axis=0)
     norms = jnp.sqrt(pltpu.roll(total, 112, 1)) / jnp.sqrt(total + 1.0)
     norm_ref[...] = norms[:, :10]
 
 
-def whole(basis, coefficients, lists, mass, damping, stiffness, eigen_row):
+def whole(count, *arrays):
+    basis = arrays[0]
     rows = basis.shape[1]
     chunks = rows // CHUNK
     subs = lax.axis_size("rows")
@@ -355,31 +383,30 @@
             jax.ShapeDtypeStruct((10, rows), jnp.bfloat16),
             jax.ShapeDtypeStruct((1, 10), jnp.float32),
         ),
-        in_specs=[pl.BlockSpec(memory_space=pltpu.HBM)] + [vmem] * 6,
-        out_specs=(vmem,) * 3,
+        in_specs=[pl.BlockSpec(memory_space=pltpu.SMEM)] + [pl.BlockSpec(memory_space=pltpu.HBM)] * 8,
+        out_specs=(pl.BlockSpec(memory_space=pltpu.HBM),) * 2 + (vmem,),
         scratch_shapes=[
+            bf16(10, rows), bf16(10, rows), *[pltpu.VMEM(a.shape, a.dtype) for a in arrays[1:]], pltpu.VMEM((2, PLANE), jnp.int32),
             bf16(1, rows), bf16(chunks, 4, 2, HALF), bf16(2, 40, 128), bf16(8, rows), bf16(2, rows),
-            bf16(8, PLANE), bf16(2, PLANE), bf16(8, PLANE), bf16(2, PLANE), pltpu.VMEM(lists.shape, jnp.int32),
+            bf16(8, PLANE), bf16(2, PLANE), bf16(8, PLANE), bf16(2, PLANE), pltpu.VMEM((2, PLANE), jnp.int32),
             bf16(chunks, 3, 4, 8, PIECE), bf16(chunks, 4, 2, HALF), bf16(chunks, 4, 8, PIECE), bf16(chunks, 4, 2, PIECE),
             f32(8, PLANE), f32(2, PLANE), f32(8, PLANE), f32(2, PLANE),
             f32(8, 128), f32(8, 128), f32(2, 128), f32(2, 128), f32(subs, 1, 128),
-            dma((chunks, 3)), dma(()), dma((2, chunks, 3, 3)), dma((2, chunks, 3)),
+            dma((2, rows // PLANE)), dma((7,)), dma((chunks, 3)), dma(()), dma((2, chunks, 3, 3)), dma((2, chunks, 3)),
             dma((2, chunks, 3)), dma((2, chunks, 3)), dma((2, 5)), dma((2, subs)),
         ],
         compiler_params=pltpu.CompilerParams(
-            collective_id=0, has_side_effects=True, vmem_limit_bytes=48 * 2**20
+            collective_id=0, has_side_effects=True, vmem_limit_bytes=67_043_328
         ),
         name="whole",
-    )(basis, coefficients, lists, mass, damping, stiffness, eigen_row)
+    )(count, *arrays)
 
 
 def on_device(basis, coefficients, eigen_values, stiffness, damping, mass, link_count, lower_cells, upper_cells):
     rows_local = basis.shape[1]
-    used = jnp.arange(lower_cells.shape[1], dtype=jnp.int32)[None, :] < link_count[0]
-    lists = jnp.where(used, jnp.concatenate([lower_cells, upper_cells], axis=0), -1)
     wide = lambda a: a.reshape(1, rows_local)
     eig, res, norms = whole(
-        basis, coefficients.T, lists, wide(mass), wide(damping), wide(stiffness), eigen_values[None, :]
+        link_count, basis, coefficients.T, lower_cells, upper_cells, wide(mass), wide(damping), wide(stiffness), eigen_values[None, :]
     )
     return eig, res, norms.reshape(10)
 

time: 83.7 us -> 81.5 us (0.974)
  local copies, waits for them, and re-layouts: 7.35 us -> 5.03 us
  Pallas kernels: 73.9 us -> 75.1 us
    unnamed x13 -> x7, local copies, waits for them, and re-layouts: 7.35 us -> 5.03 us
    pallas_call x1, Pallas kernels: 73.9 us -> 75.1 us  [whole(): pl.pallas_call(whole_kernel, out_shape=(jax.ShapeDtypeStruct((10, rows),...]
where the time goes in v4:
time: 81.5 us; the launch traced here: 81.4 us
  Pallas kernels  75.1 us (92%)
  local copies, waits for them, and re-layouts  5.03 us (6%)
  between operations  1.3 us (2%)
    pallas_call x1, Pallas kernels, whole(): pl.pallas_call(whole_kernel, out_shape=(jax.ShapeDtypeStruct((10, rows),...  75.1 us
    unnamed x7, local copies, waits for them, and re-layouts  5.03 us

profile of v4, /device:TPU:1, one launch (start us, length us, event | category | flops | bytes accessed | tf_op | source)
XLA Modules:
  0.0 81.4 jit_solution(9513177756486465612)
XLA Ops:
  1.3 75.1 %whole.1 = (bf16[10,65536]{1,0:T(8,128)(2,1)}, bf16[10,65536]{1,0:T(8,128)(2,1)}, f32[1,10]{1,0:T(1,128)}) custom-call(s32[1]{0:T(128)S(6)} %copy.15.count, bf16[25,65536]{1,0:T(8,128)(2,1)} %basis.1, bf16[40,100]{1,0:T(8,128)(2,1)} %bitcast.9, s32[1,4096]{1,0:T(1,128)} %lower_in.1, s32[1,4096]{1,0:T(1,128)} %upper_in.1, f32[1,65536]{1,0:T(1,128)} %bitcast.6, ...), custom_call_target="tpu_custom_call" | custom-call | tf_op jit(solution)/shard_map/whole/pallas_call | solution.py:379
  76.4 0.0 copy-start
  76.4 3.2 %copy.16 = bf16[10,65536]{1,0:T(8,128)(2,1)} copy(bf16[10,65536]{1,0:T(8,128)(2,1)} %get-tuple-element.12) | data formatting | bytes 2621440
  79.6 0.0 copy-done
  79.6 0.0 copy-start.1
  79.6 1.3 %copy.17 = bf16[10,65536]{1,0:T(8,128)(2,1)} copy(bf16[10,65536]{1,0:T(8,128)(2,1)S(1)} %copy-done) | data formatting | bytes 2621440
  80.9 0.0 copy-done.1
  80.9 0.5 copy.18
Async XLA Ops:
  76.4 3.2 %copy-start = (bf16[10,65536]{1,0:T(8,128)(2,1)S(1)}, bf16[10,65536]{1,0:T(8,128)(2,1)}, u32[]{:S(2)}) copy-start(bf16[10,65536]{1,0:T(8,128)(2,1)} %get-tuple-element.13) | copy-start | bytes 3932164
  79.6 1.3 %copy-start.1 = (f32[1,10]{1,0:T(1,128)S(1)}, f32[1,10]{1,0:T(1,128)}, u32[]{:S(2)}) copy-start(f32[1,10]{1,0:T(1,128)} %get-tuple-element.8) | copy-start | bytes 124

commit v5 on v4

--- a/solution.py
+++ b/solution.py
@@ -128,14 +128,15 @@
 HALF = PIECE // 2
 ORDER = (0, 7, 1, 2, 3, 4, 5, 6)
 AHEAD = 3
+LIMIT = 50_331_648
 
 
 def whole_kernel(
     count, basis, coefficients_in, lower_in, upper_in, mass_in, damping_in, stiffness_in, eigen_in,
-    eig_out, res_out, norm_ref, eig_ref, res_ref, coefficients, lower, upper, mass, damping, stiffness, eigen_row, lists,
+    eig_ref, res_ref, norm_ref, coefficients, lower, upper, mass, damping, stiffness, eigen_row, lists,
     odd_rows, extra, coefs, ea, eb, above_a, above_b, below_a, below_b, down_lists, ra, rb, sa, sb,
     first_a, first_b, last_a, last_b, square_a, residual_a, square_b, residual_b, squares,
-    output_sem, input_sem, own_sem, odd_sem, basis_sem, extra_sem, vec_a_sem, vec_b_sem, plane_sem, square_sem,
+    input_sem, own_sem, odd_sem, sent_sem, chunk_sem, plane_sem, square_recv_sem,
 ):
     me, sub = lax.axis_index("vecs"), lax.axis_index("rows")
     subs = lax.axis_size("rows")
@@ -144,6 +145,9 @@
     behind = [lax.rem(me + 4 - d, 4) for d in (1, 2, 3)]
     order = (0, 2, 1)
 
+    basis_sem, extra_sem, vec_a_sem, vec_b_sem = ((sent_sem.at[k], chunk_sem.at[k]) for k in range(4))
+    square_sem = (sent_sem.at[4], square_recv_sem)
+
     barrier = pltpu.get_barrier_semaphore()
     for peer in ahead:
         pl.semaphore_signal(barrier, inc=1, device_id={"vecs": peer}, device_id_type=MESH)
@@ -154,9 +158,12 @@
 
     def remote(source, target, sems, at, peer):
         return pltpu.make_async_remote_copy(
-            src_ref=source, dst_ref=target, send_sem=sems.at[(0, *at)], recv_sem=sems.at[(1, *at)],
+            src_ref=source, dst_ref=target, send_sem=sems[0], recv_sem=sems[1].at[at],
             device_id=peer, device_id_type=MESH,
         )
+
+    def all_of(block, sems, at=0):
+        return remote(block, block, sems, at, {"vecs": ahead[0]})
 
     def columns(c, q):
         return pl.ds(pl.multiple_of(c * CHUNK + q * PIECE, PIECE), PIECE)
@@ -166,53 +173,47 @@
             peer = ahead[d]
             for g in range(3):
                 remote(
-                    basis.at[pl.ds(8 * g, 8), columns(c, peer)], ra.at[c, g, me], basis_sem, (c, d, g), {"vecs": peer}
+                    basis.at[pl.ds(8 * g, 8), columns(c, peer)], ra.at[c, g, me], basis_sem, c, {"vecs": peer}
                 ).start()
 
     def send_extra(c):
         for d in order:
             peer = ahead[d]
-            remote(extra.at[c, peer], rb.at[c, me], extra_sem, (c, d), {"vecs": peer}).start()
+            remote(extra.at[c, peer], rb.at[c, me], extra_sem, c, {"vecs": peer}).start()
 
     def own_copies(c):
         for g in range(3):
             yield pltpu.make_async_copy(
-                basis.at[pl.ds(8 * g, 8), columns(c, me)], ra.at[c, g, me], own_sem.at[c, g]
+                basis.at[pl.ds(8 * g, 8), columns(c, me)], ra.at[c, g, me], own_sem.at[c]
             )
 
-    def basis_arrivals(c):
-        for d in order:
-            for g in range(3):
-                block = ra.at[c, g, behind[d]]
-                yield remote(block, block, basis_sem, (c, d, g), {"vecs": ahead[d]})
-            block = rb.at[c, behind[d]]
-            yield remote(block, block, extra_sem, (c, d), {"vecs": ahead[d]})
-
-    def vec_copies(c):
+    def basis_arrived(c):
+        pltpu.make_async_copy(ra.at[c, :, me], ra.at[c, :, me], own_sem.at[c]).wait()
+        all_of(ra.at[c, :, pl.ds(0, 3)], basis_sem, c).wait_recv()
+        all_of(rb.at[c, pl.ds(0, 3)], extra_sem, c).wait_recv()
+
+    def send_vecs(c):
         for d in order:
             peer = ahead[d]
-            yield remote(sa.at[c, peer], ea.at[:, columns(c, me)], vec_a_sem, (c, d), {"vecs": peer})
-            yield remote(sb.at[c, peer], eb.at[:, columns(c, me)], vec_b_sem, (c, d), {"vecs": peer})
-
-    def vec_arrivals(c):
-        for d in order:
-            block = ea.at[:, columns(c, behind[d])]
-            yield remote(block, block, vec_a_sem, (c, d), {"vecs": ahead[d]})
-            block = eb.at[:, columns(c, behind[d])]
-            yield remote(block, block, vec_b_sem, (c, d), {"vecs": ahead[d]})
+            remote(sa.at[c, peer], ea.at[:, columns(c, me)], vec_a_sem, c, {"vecs": peer}).start()
+            remote(sb.at[c, peer], eb.at[:, columns(c, me)], vec_b_sem, c, {"vecs": peer}).start()
+
+    def vecs_arrived(c):
+        all_of(sa.at[c, pl.ds(0, 3)], vec_a_sem, c).wait_recv()
+        all_of(sb.at[c, pl.ds(0, 3)], vec_b_sem, c).wait_recv()
 
     rows_local = basis.shape[1]
     plane_copies = {
         ORDER[0]: (
-            remote(ea.at[:, pl.ds(0, PLANE)], above_a, plane_sem, (0,), {"rows": previous}),
-            remote(eb.at[:, pl.ds(0, PLANE)], above_b, plane_sem, (1,), {"rows": previous}),
+            remote(ea.at[:, pl.ds(0, PLANE)], above_a, (plane_sem.at[0, 0], plane_sem.at[1]), 0, {"rows": previous}),
+            remote(eb.at[:, pl.ds(0, PLANE)], above_b, (plane_sem.at[0, 1], plane_sem.at[1]), 1, {"rows": previous}),
         ),
         ORDER[1]: (
-            remote(ea.at[:, pl.ds(rows_local - PLANE, PLANE)], below_a, plane_sem, (2,), {"rows": following}),
-            remote(eb.at[:, pl.ds(rows_local - PLANE, PLANE)], below_b, plane_sem, (3,), {"rows": following}),
+            remote(ea.at[:, pl.ds(rows_local - PLANE, PLANE)], below_a, (plane_sem.at[0, 2], plane_sem.at[1]), 2, {"rows": following}),
+            remote(eb.at[:, pl.ds(rows_local - PLANE, PLANE)], below_b, (plane_sem.at[0, 3], plane_sem.at[1]), 3, {"rows": following}),
         ),
     }
-    list_copy = remote(lists, down_lists, plane_sem, (4,), {"rows": following})
+    list_copy = remote(lists, down_lists, (plane_sem.at[0, 4], plane_sem.at[1]), 4, {"rows": following})
 
     inputs = [
         pltpu.make_async_copy(source, target, input_sem.at[i])
@@ -257,15 +258,8 @@
     for copy in inputs[4:]:
         copy.wait()
 
-    output_copies = []
-
     def planes_done(first, planes, links=None):
         residual_spans((ea, eb), (eig_ref, res_ref), diag_refs, eigen, first, planes, links, sums)
-        at = pl.ds(first * PLANE, planes * PLANE)
-        for k, (held, out) in enumerate(((eig_ref, eig_out), (res_ref, res_out))):
-            copy = pltpu.make_async_copy(held.at[:, at], out.at[:, at], output_sem.at[k, first])
-            copy.start()
-            output_copies.append(copy)
 
     def product(c):
         for h in range(2):
@@ -283,8 +277,7 @@
         eb[:, columns(c, me)] = sb[c, me]
 
     def arrived(c):
-        for copy in vec_arrivals(c):
-            copy.wait_recv()
+        vecs_arrived(c)
         for copy in plane_copies.get(c, ()):
             copy.start()
 
@@ -305,13 +298,9 @@
 
     later = {5: first_links, 6: last_links, 7: outer_planes}
     for i, c in enumerate(ORDER):
-        for copy in own_copies(c):
-            copy.wait()
-        for copy in basis_arrivals(c):
-            copy.wait_recv()
+        basis_arrived(c)
         product(c)
-        for copy in vec_copies(c):
-            copy.start()
+        send_vecs(c)
         if i + AHEAD < len(ORDER):
             send_basis(ORDER[i + AHEAD])
             send_extra(ORDER[i + AHEAD])
@@ -334,34 +323,22 @@
         message = message + jnp.sum(jnp.where(row == lane, column, 0.0), axis=0, keepdims=True)
     squares[sub] = message
 
-    def square_copy(d):
-        return remote(squares.at[sub], squares.at[sub], square_sem, (d,), {"rows": lax.rem(sub + d, subs)})
-
     @pl.loop(1, subs)
     def _(d):
-        square_copy(d).start()
+        remote(squares.at[sub], squares.at[sub], square_sem, 0, {"rows": lax.rem(sub + d, subs)}).start()
 
     for copies in plane_copies.values():
         for copy in copies:
             copy.wait_send()
     list_copy.wait_send()
-    for c in ORDER:
-        for copy in basis_arrivals(c):
-            copy.wait_send()
-        for copy in vec_copies(c):
-            copy.wait_send()
-
-    @pl.loop(1, subs)
-    def _(d):
-        block = squares.at[lax.rem(sub + subs - d, subs)]
-        remote(block, block, square_sem, (d,), {"rows": lax.rem(sub + d, subs)}).wait_recv()
-
-    @pl.loop(1, subs)
-    def _(d):
-        square_copy(d).wait_send()
-
-    for copy in output_copies:
-        copy.wait()
+    all_of(ra.at[:, :, pl.ds(0, 3)], basis_sem).wait_send()
+    all_of(rb.at[:, pl.ds(0, 3)], extra_sem).wait_send()
+    all_of(sa.at[:, pl.ds(0, 3)], vec_a_sem).wait_send()
+    all_of(sb.at[:, pl.ds(0, 3)], vec_b_sem).wait_send()
+
+    every = squares.at[pl.ds(0, subs - 1)]
+    all_of(every, square_sem).wait_recv()
+    all_of(every, square_sem).wait_send()
     total = jnp.sum(squares[...], axis=0)
     norms = jnp.sqrt(pltpu.roll(total, 112, 1)) / jnp.sqrt(total + 1.0)
     norm_ref[...] = norms[:, :10]
@@ -384,22 +361,21 @@
             jax.ShapeDtypeStruct((1, 10), jnp.float32),
         ),
         in_specs=[pl.BlockSpec(memory_space=pltpu.SMEM)] + [pl.BlockSpec(memory_space=pltpu.HBM)] * 8,
-        out_specs=(pl.BlockSpec(memory_space=pltpu.HBM),) * 2 + (vmem,),
+        out_specs=(vmem,) * 3,
         scratch_shapes=[
-            bf16(10, rows), bf16(10, rows), *[pltpu.VMEM(a.shape, a.dtype) for a in arrays[1:]], pltpu.VMEM((2, PLANE), jnp.int32),
+            *[pltpu.VMEM(a.shape, a.dtype) for a in arrays[1:]], pltpu.VMEM((2, PLANE), jnp.int32),
             bf16(1, rows), bf16(chunks, 4, 2, HALF), bf16(2, 40, 128), bf16(8, rows), bf16(2, rows),
             bf16(8, PLANE), bf16(2, PLANE), bf16(8, PLANE), bf16(2, PLANE), pltpu.VMEM((2, PLANE), jnp.int32),
             bf16(chunks, 3, 4, 8, PIECE), bf16(chunks, 4, 2, HALF), bf16(chunks, 4, 8, PIECE), bf16(chunks, 4, 2, PIECE),
             f32(8, PLANE), f32(2, PLANE), f32(8, PLANE), f32(2, PLANE),
             f32(8, 128), f32(8, 128), f32(2, 128), f32(2, 128), f32(subs, 1, 128),
-            dma((2, rows // PLANE)), dma((7,)), dma((chunks, 3)), dma(()), dma((2, chunks, 3, 3)), dma((2, chunks, 3)),
-            dma((2, chunks, 3)), dma((2, chunks, 3)), dma((2, 5)), dma((2, subs)),
+            dma((7,)), dma((chunks,)), dma(()), dma((5,)), dma((4, chunks)), dma((2, 5)), dma((1,)),
         ],
         compiler_params=pltpu.CompilerParams(
-            collective_id=0, has_side_effects=True, vmem_limit_bytes=67_043_328
+            collective_id=0, has_side_effects=True, vmem_limit_bytes=LIMIT
         ),
         name="whole",
-    )(count, *arrays)
+    )(count, *[pltpu.with_memory_space_constraint(a, pltpu.HBM) for a in arrays])
 
 
 def on_device(basis, coefficients, eigen_values, stiffness, damping, mass, link_count, lower_cells, upper_cells):

time: 81.5 us -> 75.6 us (0.928)
  Pallas kernels: 75.1 us -> 71 us
  local copies, waits for them, and re-layouts: 5.03 us -> 3.15 us
    pallas_call x1, Pallas kernels: 75.1 us -> 71 us  [whole(): pl.pallas_call(whole_kernel, out_shape=(jax.ShapeDtypeStruct((10, rows),...]
    unnamed x7 -> x3, local copies, waits for them, and re-layouts: 5.03 us -> 3.15 us
where the time goes in v5:
time: 75.6 us; the launch traced here: 75.4 us
  Pallas kernels  71 us (94%)
  local copies, waits for them, and re-layouts  3.15 us (4%)
  between operations  1.29 us (2%)
    pallas_call x1, Pallas kernels, whole(): pl.pallas_call(whole_kernel, out_shape=(jax.ShapeDtypeStruct((10, rows),...  71 us
    unnamed x3, local copies, waits for them, and re-layouts  3.15 us

profile of v5, /device:TPU:1, one launch (start us, length us, event | category | flops | bytes accessed | tf_op | source)
XLA Modules:
  0.0 75.4 jit_solution(8328558076412468443)
XLA Ops:
  1.3 71.0 %whole.1 = (bf16[10,65536]{1,0:T(8,128)(2,1)S(1)}, bf16[10,65536]{1,0:T(8,128)(2,1)S(1)}, f32[1,10]{1,0:T(1,128)S(1)}) custom-call(s32[1]{0:T(128)S(6)} %copy.15.count, bf16[25,65536]{1,0:T(8,128)(2,1)} %basis.1, bf16[40,100]{1,0:T(8,128)(2,1)} %bitcast.10, s32[1,4096]{1,0:T(1,128)} %lower_in.1, s32[1,4096]{1,0:T(1,128)} %upper_in.1, f32[1,65536]{1,0:T(1,128)} %bitcast.7, ...), custom_call_target="tpu_custom_call" | custom-call | tf_op jit(solution)/shard_map/whole/pallas_call | solution.py:356
  72.3 1.3 %copy.16 = bf16[10,65536]{1,0:T(8,128)(2,1)} copy(bf16[10,65536]{1,0:T(8,128)(2,1)S(1)} %get-tuple-element.12) | data formatting | bytes 2621440
  73.6 1.3 %copy.17 = bf16[10,65536]{1,0:T(8,128)(2,1)} copy(bf16[10,65536]{1,0:T(8,128)(2,1)S(1)} %get-tuple-element.13) | data formatting | bytes 2621440
  74.9 0.5 copy.18

commit v6 on v5

--- a/solution.py
+++ b/solution.py
@@ -105,21 +105,44 @@
     return jnp.sum(jnp.where(same, row, 0.0), axis=1, keepdims=True)
 
 
-def spread_coefficients(coefficients, coefs):
+def spread_coefficients(coefficients, coefs, devices, which):
     out = lax.broadcasted_iota(jnp.int32, (40, 40), 0)
     vec = lax.broadcasted_iota(jnp.int32, (40, 40), 1)
     rest = out - 32
-    wanted = jnp.where(out < 32, 10 * (out >> 3) + (out & 7), 10 * (rest >> 1) + 8 + (rest & 1))
-    rows = jnp.where(vec == wanted, 1.0, 0.0).astype(jnp.bfloat16)
+    group = jnp.where(out < 32, out >> 3, rest >> 1)
+    place = jnp.where(out < 32, out & 7, 8 + (rest & 1))
+    owner = devices[3]
+    for k in range(3):
+        owner = jnp.where(group == k, devices[k], owner)
+    rows = jnp.where(vec == 10 * owner + place, 1.0, 0.0).astype(jnp.bfloat16)
     ordered = jnp.dot(rows, coefficients[...], preferred_element_type=jnp.float32).astype(jnp.bfloat16)
-    rank = lax.broadcasted_iota(jnp.int32, (100, 128), 0)
-    at = lax.broadcasted_iota(jnp.int32, (100, 128), 1)
-    odd = at - 96
+    rank = lax.broadcasted_iota(jnp.int32, (100, 64), 0)
+    at = lax.broadcasted_iota(jnp.int32, (100, 64), 1)
+    odd = at - 48
     for h in range(2):
-        main = 25 * ((at >> 3) & 3) + 8 * (at >> 5) + (at & 7)
-        other = jnp.where((odd < 8) & ((odd & 1) == h), 25 * (odd >> 1) + 24, -1)
-        pick = jnp.where(rank == jnp.where(at < 96, main, other), 1.0, 0.0).astype(jnp.bfloat16)
-        coefs[h] = jnp.dot(ordered, pick, preferred_element_type=jnp.float32).astype(jnp.bfloat16)
+        main = 25 * jnp.where(((at >> 3) & 1) == 0, devices[0], devices[1]) + 8 * (at >> 4) + (at & 7)
+        other = 25 * jnp.where((odd >> 1) == 0, devices[0], devices[1]) + 24
+        other = jnp.where((odd < 4) & ((odd & 1) == h), other, -1)
+        pick = jnp.where(rank == jnp.where(at < 48, main, other), 1.0, 0.0).astype(jnp.bfloat16)
+        coefs[which, h] = jnp.dot(ordered, pick, preferred_element_type=jnp.float32).astype(jnp.bfloat16)
+
+
+STEPS = 32760.0
+
+
+def send_scaled(parts, target):
+    top = jnp.max(jnp.concatenate([jnp.abs(part) for part in parts], axis=1), axis=1, keepdims=True)
+    power = jnp.ceil(jnp.log2(jnp.maximum(top, 1e-30)))
+    factor = jnp.exp2(-power) * STEPS
+    for h, part in enumerate(parts):
+        target[:, h * HALF : (h + 1) * HALF] = jnp.round(part * factor).astype(jnp.int32).astype(jnp.int16)
+    wide = jnp.broadcast_to(power, (power.shape[0], 128))
+    target[:, PIECE : PIECE + 128] = wide.astype(jnp.int32).astype(jnp.int16)
+
+
+def scaled_back(source, h):
+    power = source[:, PIECE : PIECE + 128].astype(jnp.int32).astype(jnp.float32)[:, :1]
+    return source[:, h * HALF : (h + 1) * HALF].astype(jnp.int32).astype(jnp.float32) * (jnp.exp2(power) * (1.0 / STEPS))
 
 
 MESH = pl.DeviceIdType.MESH
@@ -127,29 +150,31 @@
 CHUNK = 4 * PIECE
 HALF = PIECE // 2
 ORDER = (0, 7, 1, 2, 3, 4, 5, 6)
-AHEAD = 3
+AHEAD = 2
 LIMIT = 50_331_648
 
 
 def whole_kernel(
     count, basis, coefficients_in, lower_in, upper_in, mass_in, damping_in, stiffness_in, eigen_in,
     eig_ref, res_ref, norm_ref, coefficients, lower, upper, mass, damping, stiffness, eigen_row, lists,
-    odd_rows, extra, coefs, ea, eb, above_a, above_b, below_a, below_b, down_lists, ra, rb, sa, sb,
+    odd_rows, extra, coefs, ea, eb, above_a, above_b, below_a, below_b, down_lists, ra, rb,
+    part_a, part_b, to_a, to_b, from_a, from_b, mate_a, mate_b,
     first_a, first_b, last_a, last_b, square_a, residual_a, square_b, residual_b, squares,
     input_sem, own_sem, odd_sem, sent_sem, chunk_sem, plane_sem, square_recv_sem,
 ):
     me, sub = lax.axis_index("vecs"), lax.axis_index("rows")
     subs = lax.axis_size("rows")
     following, previous = lax.rem(sub + 1, subs), lax.rem(sub + subs - 1, subs)
-    ahead = [lax.rem(me + d, 4) for d in (1, 2, 3)]
-    behind = [lax.rem(me + 4 - d, 4) for d in (1, 2, 3)]
-    order = (0, 2, 1)
-
-    basis_sem, extra_sem, vec_a_sem, vec_b_sem = ((sent_sem.at[k], chunk_sem.at[k]) for k in range(4))
-    square_sem = (sent_sem.at[4], square_recv_sem)
+    one, two = me + 1 - 2 * lax.rem(me, 2), 3 - me
+    mates, crosses = (one, two), (two, one)
+    halves = (lax.rem(lax.div(me + 1, 2), 2), lax.div(me, 2))
+    basis_sem, extra_sem, sum_a_sem, sum_b_sem, vec_a_sem, vec_b_sem = (
+        (sent_sem.at[k], chunk_sem.at[k]) for k in range(6)
+    )
+    square_sem = (sent_sem.at[6], square_recv_sem)
 
     barrier = pltpu.get_barrier_semaphore()
-    for peer in ahead:
+    for peer in mates:
         pl.semaphore_signal(barrier, inc=1, device_id={"vecs": peer}, device_id_type=MESH)
 
     @pl.loop(1, subs)
@@ -163,44 +188,47 @@
         )
 
     def all_of(block, sems, at=0):
-        return remote(block, block, sems, at, {"vecs": ahead[0]})
-
-    def columns(c, q):
-        return pl.ds(pl.multiple_of(c * CHUNK + q * PIECE, PIECE), PIECE)
+        return remote(block, block, sems, at, {"vecs": one})
+
+    def columns(c, x, half):
+        return pl.ds(pl.multiple_of(c * CHUNK + x * PLANE + half * PIECE, PIECE), PIECE)
 
     def send_basis(c):
-        for d in order:
-            peer = ahead[d]
+        for x, (mate, half) in enumerate(zip(mates, halves)):
             for g in range(3):
                 remote(
-                    basis.at[pl.ds(8 * g, 8), columns(c, peer)], ra.at[c, g, me], basis_sem, c, {"vecs": peer}
+                    basis.at[pl.ds(8 * g, 8), columns(c, x, 1 - half)], ra.at[c, x, g, 1], basis_sem, c, {"vecs": mate}
                 ).start()
 
     def send_extra(c):
-        for d in order:
-            peer = ahead[d]
-            remote(extra.at[c, peer], rb.at[c, me], extra_sem, c, {"vecs": peer}).start()
+        for x, (mate, half) in enumerate(zip(mates, halves)):
+            remote(extra.at[c, 2 * x + 1 - half], rb.at[c, x, 1], extra_sem, c, {"vecs": mate}).start()
 
     def own_copies(c):
-        for g in range(3):
-            yield pltpu.make_async_copy(
-                basis.at[pl.ds(8 * g, 8), columns(c, me)], ra.at[c, g, me], own_sem.at[c]
-            )
+        for x, half in enumerate(halves):
+            for g in range(3):
+                yield pltpu.make_async_copy(
+                    basis.at[pl.ds(8 * g, 8), columns(c, x, half)], ra.at[c, x, g, 0], own_sem.at[c]
+                )
 
     def basis_arrived(c):
-        pltpu.make_async_copy(ra.at[c, :, me], ra.at[c, :, me], own_sem.at[c]).wait()
-        all_of(ra.at[c, :, pl.ds(0, 3)], basis_sem, c).wait_recv()
-        all_of(rb.at[c, pl.ds(0, 3)], extra_sem, c).wait_recv()
+        pltpu.make_async_copy(ra.at[c, :, :, 0], ra.at[c, :, :, 0], own_sem.at[c]).wait()
+        all_of(ra.at[c, :, :, 1], basis_sem, c).wait_recv()
+        all_of(rb.at[c, :, 1], extra_sem, c).wait_recv()
+
+    def send_sums(c):
+        for x, cross in enumerate(crosses):
+            remote(to_a.at[c, x], from_a.at[c, x], sum_a_sem, c, {"vecs": cross}).start()
+            remote(to_b.at[c, x], from_b.at[c, x], sum_b_sem, c, {"vecs": cross}).start()
 
     def send_vecs(c):
-        for d in order:
-            peer = ahead[d]
-            remote(sa.at[c, peer], ea.at[:, columns(c, me)], vec_a_sem, c, {"vecs": peer}).start()
-            remote(sb.at[c, peer], eb.at[:, columns(c, me)], vec_b_sem, c, {"vecs": peer}).start()
+        for x, (mate, half) in enumerate(zip(mates, halves)):
+            remote(mate_a.at[c, x], ea.at[:, columns(c, x, half)], vec_a_sem, c, {"vecs": mate}).start()
+            remote(mate_b.at[c, x], eb.at[:, columns(c, x, half)], vec_b_sem, c, {"vecs": mate}).start()
 
     def vecs_arrived(c):
-        all_of(sa.at[c, pl.ds(0, 3)], vec_a_sem, c).wait_recv()
-        all_of(sb.at[c, pl.ds(0, 3)], vec_b_sem, c).wait_recv()
+        all_of(mate_a.at[c], vec_a_sem, c).wait_recv()
+        all_of(mate_b.at[c], vec_b_sem, c).wait_recv()
 
     rows_local = basis.shape[1]
     plane_copies = {
@@ -232,11 +260,13 @@
         copy.start()
     for copy in inputs[:4]:
         copy.wait()
-    spread_coefficients(coefficients, coefs)
+    for x in range(2):
+        devices = (me, mates[x], crosses[x], 6 - me - one - two)
+        spread_coefficients(coefficients, coefs, devices, x)
     used = lax.broadcasted_iota(jnp.int32, (1, PLANE), 1) < count[0]
     lists[0:1, :] = jnp.where(used, lower[...], -1)
     lists[1:2, :] = jnp.where(used, upper[...], -1)
-    pl.semaphore_wait(barrier, subs + 2)
+    pl.semaphore_wait(barrier, subs + 1)
     for c in ORDER[:AHEAD]:
         send_basis(c)
     odd_copy.wait()
@@ -246,7 +276,8 @@
             pair = [odd_rows[0:1, at + h * HALF : at + (h + 1) * HALF].astype(jnp.float32) for h in range(2)]
             extra[c, q] = jnp.concatenate(pair, axis=0).astype(jnp.bfloat16)
     for c in ORDER:
-        rb[c, me] = extra[c, me]
+        for x, half in enumerate(halves):
+            rb[c, x, 0] = extra[c, 2 * x + half]
     for c in ORDER[:AHEAD]:
         send_extra(c)
     list_copy.start()
@@ -262,19 +293,36 @@
         residual_spans((ea, eb), (eig_ref, res_ref), diag_refs, eigen, first, planes, links, sums)
 
     def product(c):
-        for h in range(2):
-            at = pl.ds(h * HALF, HALF)
-            parts = [ra[c, g, :, :, at].reshape(32, HALF) for g in range(3)]
-            odd = jnp.concatenate(
-                [rb[c, q].astype(jnp.float32) for q in range(4)] + [jnp.zeros((24, HALF), jnp.float32)], axis=0
-            )
-            whole = jnp.concatenate([*parts, odd.astype(jnp.bfloat16)], axis=0)
-            out = jnp.dot(coefs[h], whole, preferred_element_type=jnp.float32)
-            for p in range(4):
-                sa[c, p, :, at] = out[8 * p : 8 * p + 8].astype(jnp.bfloat16)
-                sb[c, p, :, at] = out[32 + 2 * p : 34 + 2 * p].astype(jnp.bfloat16)
-        ea[:, columns(c, me)] = sa[c, me]
-        eb[:, columns(c, me)] = sb[c, me]
+        for x in range(2):
+            outs = []
+            for h in range(2):
+                at = pl.ds(h * HALF, HALF)
+                parts = [ra[c, x, g, :, :, at].reshape(16, HALF) for g in range(3)]
+                odd = jnp.concatenate(
+                    [rb[c, x, q].astype(jnp.float32) for q in range(2)] + [jnp.zeros((12, HALF), jnp.float32)], axis=0
+                )
+                stack = jnp.concatenate([*parts, odd.astype(jnp.bfloat16)], axis=0)
+                out = jnp.dot(coefs[x, h], stack, preferred_element_type=jnp.float32)
+                part_a[c, x, :, at] = out[0:16]
+                part_b[c, x, :, at] = out[32:36]
+                outs.append(out)
+            send_scaled([out[16:32] for out in outs], to_a.at[c, x])
+            send_scaled([out[36:40] for out in outs], to_b.at[c, x])
+
+    def combine(c):
+        all_of(from_a.at[c], sum_a_sem, c).wait_recv()
+        all_of(from_b.at[c], sum_b_sem, c).wait_recv()
+        for x, half in enumerate(halves):
+            for h in range(2):
+                at = pl.ds(h * HALF, HALF)
+                here = pl.ds(pl.multiple_of(c * CHUNK + x * PLANE + half * PIECE + h * HALF, HALF), HALF)
+                vecs = (part_a[c, x, :, at] + scaled_back(from_a.at[c, x], h)).astype(jnp.bfloat16)
+                ea[:, here] = vecs[:8]
+                mate_a[c, x, :, at] = vecs[8:]
+                vecs = (part_b[c, x, :, at] + scaled_back(from_b.at[c, x], h)).astype(jnp.bfloat16)
+                eb[:, here] = vecs[:2]
+                mate_b[c, x, :, at] = vecs[2:]
+        send_vecs(c)
 
     def arrived(c):
         vecs_arrived(c)
@@ -296,20 +344,26 @@
         planes_done(0, 1, (first_a, first_b))
         planes_done(rows_local // PLANE - 1, 1, (last_a, last_b))
 
-    later = {5: first_links, 6: last_links, 7: outer_planes}
+    later = {6: first_links, 7: last_links}
     for i, c in enumerate(ORDER):
         basis_arrived(c)
         product(c)
-        send_vecs(c)
+        send_sums(c)
         if i + AHEAD < len(ORDER):
             send_basis(ORDER[i + AHEAD])
             send_extra(ORDER[i + AHEAD])
-        if i >= 2:
-            arrived(ORDER[i - 2])
-            if i >= 4:
-                planes_done(2 * ORDER[i - 2] - 1, 2)
+        if i >= 1:
+            combine(ORDER[i - 1])
+        if i >= 3:
+            arrived(ORDER[i - 3])
+            if i >= 5:
+                planes_done(2 * ORDER[i - 3] - 1, 2)
         if i in later:
             later[i]()
+    combine(ORDER[-1])
+    outer_planes()
+    arrived(ORDER[-3])
+    planes_done(2 * ORDER[-3] - 1, 2)
     arrived(ORDER[-2])
     planes_done(2 * ORDER[-2] - 1, 2)
     arrived(ORDER[-1])
@@ -331,11 +385,12 @@
         for copy in copies:
             copy.wait_send()
     list_copy.wait_send()
-    all_of(ra.at[:, :, pl.ds(0, 3)], basis_sem).wait_send()
-    all_of(rb.at[:, pl.ds(0, 3)], extra_sem).wait_send()
-    all_of(sa.at[:, pl.ds(0, 3)], vec_a_sem).wait_send()
-    all_of(sb.at[:, pl.ds(0, 3)], vec_b_sem).wait_send()
-
+    all_of(ra.at[:, :, :, 1], basis_sem).wait_send()
+    all_of(rb.at[:, :, 1], extra_sem).wait_send()
+    all_of(from_a, sum_a_sem).wait_send()
+    all_of(from_b, sum_b_sem).wait_send()
+    all_of(mate_a, vec_a_sem).wait_send()
+    all_of(mate_b, vec_b_sem).wait_send()
     every = squares.at[pl.ds(0, subs - 1)]
     all_of(every, square_sem).wait_recv()
     all_of(every, square_sem).wait_send()
@@ -364,12 +419,15 @@
         out_specs=(vmem,) * 3,
         scratch_shapes=[
             *[pltpu.VMEM(a.shape, a.dtype) for a in arrays[1:]], pltpu.VMEM((2, PLANE), jnp.int32),
-            bf16(1, rows), bf16(chunks, 4, 2, HALF), bf16(2, 40, 128), bf16(8, rows), bf16(2, rows),
+            bf16(1, rows), bf16(chunks, 4, 2, HALF), bf16(2, 2, 40, 64), bf16(8, rows), bf16(2, rows),
             bf16(8, PLANE), bf16(2, PLANE), bf16(8, PLANE), bf16(2, PLANE), pltpu.VMEM((2, PLANE), jnp.int32),
-            bf16(chunks, 3, 4, 8, PIECE), bf16(chunks, 4, 2, HALF), bf16(chunks, 4, 8, PIECE), bf16(chunks, 4, 2, PIECE),
+            bf16(chunks, 2, 3, 2, 8, PIECE), bf16(chunks, 2, 2, 2, HALF),
+            f32(chunks, 2, 16, PIECE), f32(chunks, 2, 4, PIECE),
+            *[pltpu.VMEM((chunks, 2, r, PIECE + 128), jnp.int16) for r in (16, 4, 16, 4)],
+            bf16(chunks, 2, 8, PIECE), bf16(chunks, 2, 2, PIECE),
             f32(8, PLANE), f32(2, PLANE), f32(8, PLANE), f32(2, PLANE),
             f32(8, 128), f32(8, 128), f32(2, 128), f32(2, 128), f32(subs, 1, 128),
-            dma((7,)), dma((chunks,)), dma(()), dma((5,)), dma((4, chunks)), dma((2, 5)), dma((1,)),
+            dma((7,)), dma((chunks,)), dma(()), dma((7,)), dma((6, chunks)), dma((2, 5)), dma((1,)),
         ],
         compiler_params=pltpu.CompilerParams(
             collective_id=0, has_side_effects=True, vmem_limit_bytes=LIMIT

time: 75.6 us -> 70.8 us (0.937)
  Pallas kernels: 71 us -> 66.2 us
    pallas_call x1, Pallas kernels: 71 us -> 66.2 us  [whole(): pl.pallas_call(whole_kernel, out_shape=(jax.ShapeDtypeStruct((10, rows),...]
where the time goes in v6:
time: 70.8 us; the launch traced here: 70.6 us
  Pallas kernels  66.2 us (94%)
  local copies, waits for them, and re-layouts  3.15 us (4%)
  between operations  1.29 us (2%)
    pallas_call x1, Pallas kernels, whole(): pl.pallas_call(whole_kernel, out_shape=(jax.ShapeDtypeStruct((10, rows),...  66.2 us
    unnamed x3, local copies, waits for them, and re-layouts  3.15 us

profile of v6, /device:TPU:1, one launch (start us, length us, event | category | flops | bytes accessed | tf_op | source)
XLA Modules:
  0.0 70.6 jit_solution(12531471717126413039)
XLA Ops:
  1.3 66.2 %whole.1 = (bf16[10,65536]{1,0:T(8,128)(2,1)S(1)}, bf16[10,65536]{1,0:T(8,128)(2,1)S(1)}, f32[1,10]{1,0:T(1,128)S(1)}) custom-call(s32[1]{0:T(128)S(6)} %copy.15.count, bf16[25,65536]{1,0:T(8,128)(2,1)} %basis.1, bf16[40,100]{1,0:T(8,128)(2,1)} %bitcast.10, s32[1,4096]{1,0:T(1,128)} %lower_in.1, s32[1,4096]{1,0:T(1,128)} %upper_in.1, f32[1,65536]{1,0:T(1,128)} %bitcast.7, ...), custom_call_target="tpu_custom_call" | custom-call | tf_op jit(solution)/shard_map/whole/pallas_call | solution.py:411
  67.5 1.3 %copy.16 = bf16[10,65536]{1,0:T(8,128)(2,1)} copy(bf16[10,65536]{1,0:T(8,128)(2,1)S(1)} %get-tuple-element.12) | data formatting | bytes 2621440
  68.8 1.3 %copy.17 = bf16[10,65536]{1,0:T(8,128)(2,1)} copy(bf16[10,65536]{1,0:T(8,128)(2,1)S(1)} %get-tuple-element.13) | data formatting | bytes 2621440
  70.1 0.5 copy.18

commit v7 on v6

--- a/solution.py
+++ b/solution.py
@@ -120,7 +120,7 @@
     at = lax.broadcasted_iota(jnp.int32, (100, 64), 1)
     odd = at - 48
     for h in range(2):
-        main = 25 * jnp.where(((at >> 3) & 1) == 0, devices[0], devices[1]) + 8 * (at >> 4) + (at & 7)
+        main = jnp.where(at < 24, 25 * devices[0] + at, 25 * devices[1] + at - 24)
         other = 25 * jnp.where((odd >> 1) == 0, devices[0], devices[1]) + 24
         other = jnp.where((odd < 4) & ((odd & 1) == h), other, -1)
         pick = jnp.where(rank == jnp.where(at < 48, main, other), 1.0, 0.0).astype(jnp.bfloat16)
@@ -130,19 +130,20 @@
 STEPS = 32760.0
 
 
-def send_scaled(parts, target):
-    top = jnp.max(jnp.concatenate([jnp.abs(part) for part in parts], axis=1), axis=1, keepdims=True)
-    power = jnp.ceil(jnp.log2(jnp.maximum(top, 1e-30)))
-    factor = jnp.exp2(-power) * STEPS
-    for h, part in enumerate(parts):
-        target[:, h * HALF : (h + 1) * HALF] = jnp.round(part * factor).astype(jnp.int32).astype(jnp.int16)
-    wide = jnp.broadcast_to(power, (power.shape[0], 128))
-    target[:, PIECE : PIECE + 128] = wide.astype(jnp.int32).astype(jnp.int16)
-
-
-def scaled_back(source, h):
-    power = source[:, PIECE : PIECE + 128].astype(jnp.int32).astype(jnp.float32)[:, :1]
-    return source[:, h * HALF : (h + 1) * HALF].astype(jnp.int32).astype(jnp.float32) * (jnp.exp2(power) * (1.0 / STEPS))
+def send_scaled(blocks, target):
+    lane = lax.broadcasted_iota(jnp.int32, (8, 128), 1)
+    powers, at = jnp.zeros((8, 128), jnp.float32), 0
+    for k, parts in enumerate(blocks):
+        top = jnp.max(jnp.abs(parts[0]), axis=1, keepdims=True)
+        for part in parts[1:]:
+            top = jnp.maximum(top, jnp.max(jnp.abs(part), axis=1, keepdims=True))
+        power = jnp.ceil(jnp.log2(jnp.maximum(top, 1e-30)))
+        powers = jnp.where(lane == k, power, powers)
+        factor = jnp.exp2(-power) * STEPS
+        for part in parts:
+            target[:, at : at + HALF] = jnp.round(part * factor).astype(jnp.int32).astype(jnp.int16)
+            at += HALF
+    target[:, at : at + 128] = powers.astype(jnp.int32).astype(jnp.int16)
 
 
 MESH = pl.DeviceIdType.MESH
@@ -151,6 +152,8 @@
 HALF = PIECE // 2
 ORDER = (0, 7, 1, 2, 3, 4, 5, 6)
 AHEAD = 2
+SUMS_LAG, VECS_LAG = 1, 2
+OUTER = 7
 LIMIT = 50_331_648
 
 
@@ -158,7 +161,7 @@
     count, basis, coefficients_in, lower_in, upper_in, mass_in, damping_in, stiffness_in, eigen_in,
     eig_ref, res_ref, norm_ref, coefficients, lower, upper, mass, damping, stiffness, eigen_row, lists,
     odd_rows, extra, coefs, ea, eb, above_a, above_b, below_a, below_b, down_lists, ra, rb,
-    part_a, part_b, to_a, to_b, from_a, from_b, mate_a, mate_b,
+    part_a, part_b, to_sums, from_sums, mate_a, mate_b,
     first_a, first_b, last_a, last_b, square_a, residual_a, square_b, residual_b, squares,
     input_sem, own_sem, odd_sem, sent_sem, chunk_sem, plane_sem, square_recv_sem,
 ):
@@ -168,10 +171,10 @@
     one, two = me + 1 - 2 * lax.rem(me, 2), 3 - me
     mates, crosses = (one, two), (two, one)
     halves = (lax.rem(lax.div(me + 1, 2), 2), lax.div(me, 2))
-    basis_sem, extra_sem, sum_a_sem, sum_b_sem, vec_a_sem, vec_b_sem = (
-        (sent_sem.at[k], chunk_sem.at[k]) for k in range(6)
+    basis_sem, extra_sem, sum_sem, vec_a_sem, vec_b_sem = (
+        (sent_sem.at[k], chunk_sem.at[k]) for k in range(5)
     )
-    square_sem = (sent_sem.at[6], square_recv_sem)
+    square_sem = (sent_sem.at[5], square_recv_sem)
 
     barrier = pltpu.get_barrier_semaphore()
     for peer in mates:
@@ -191,35 +194,29 @@
         return remote(block, block, sems, at, {"vecs": one})
 
     def columns(c, x, half):
-        return pl.ds(pl.multiple_of(c * CHUNK + x * PLANE + half * PIECE, PIECE), PIECE)
+        return pl.ds(pl.multiple_of(c * CHUNK + x * CHUNK // 2 + half * PIECE, PIECE), PIECE)
 
     def send_basis(c):
         for x, (mate, half) in enumerate(zip(mates, halves)):
-            for g in range(3):
-                remote(
-                    basis.at[pl.ds(8 * g, 8), columns(c, x, 1 - half)], ra.at[c, x, g, 1], basis_sem, c, {"vecs": mate}
-                ).start()
-
-    def send_extra(c):
+            remote(
+                basis.at[pl.ds(0, 24), columns(c, x, 1 - half)], ra.at[c, x, 1], basis_sem, c, {"vecs": mate}
+            ).start()
+
+    def send_extra():
         for x, (mate, half) in enumerate(zip(mates, halves)):
-            remote(extra.at[c, 2 * x + 1 - half], rb.at[c, x, 1], extra_sem, c, {"vecs": mate}).start()
+            remote(extra.at[x, 1 - half], rb.at[x, 1], extra_sem, 0, {"vecs": mate}).start()
 
     def own_copies(c):
         for x, half in enumerate(halves):
-            for g in range(3):
-                yield pltpu.make_async_copy(
-                    basis.at[pl.ds(8 * g, 8), columns(c, x, half)], ra.at[c, x, g, 0], own_sem.at[c]
-                )
+            yield pltpu.make_async_copy(basis.at[pl.ds(0, 24), columns(c, x, half)], ra.at[c, x, 0], own_sem.at[c])
 
     def basis_arrived(c):
-        pltpu.make_async_copy(ra.at[c, :, :, 0], ra.at[c, :, :, 0], own_sem.at[c]).wait()
-        all_of(ra.at[c, :, :, 1], basis_sem, c).wait_recv()
-        all_of(rb.at[c, :, 1], extra_sem, c).wait_recv()
+        pltpu.make_async_copy(ra.at[c, :, 0], ra.at[c, :, 0], own_sem.at[c]).wait()
+        all_of(ra.at[c, :, 1], basis_sem, c).wait_recv()
 
     def send_sums(c):
         for x, cross in enumerate(crosses):
-            remote(to_a.at[c, x], from_a.at[c, x], sum_a_sem, c, {"vecs": cross}).start()
-            remote(to_b.at[c, x], from_b.at[c, x], sum_b_sem, c, {"vecs": cross}).start()
+            remote(to_sums.at[c, x], from_sums.at[c, x], sum_sem, c, {"vecs": cross}).start()
 
     def send_vecs(c):
         for x, (mate, half) in enumerate(zip(mates, halves)):
@@ -258,6 +255,18 @@
             copy.start()
     for copy in inputs[1:]:
         copy.start()
+    pl.semaphore_wait(barrier, subs + 1)
+    for c in ORDER[:AHEAD]:
+        send_basis(c)
+    odd_copy.wait()
+    for c in ORDER:
+        for q in range(4):
+            at = c * CHUNK + q * PIECE
+            pair = [odd_rows[0:1, at + h * HALF : at + (h + 1) * HALF].astype(jnp.float32) for h in range(2)]
+            extra[q // 2, q % 2, c] = jnp.concatenate(pair, axis=0).astype(jnp.bfloat16)
+    for x, half in enumerate(halves):
+        rb[x, 0] = extra[x, half]
+    send_extra()
     for copy in inputs[:4]:
         copy.wait()
     for x in range(2):
@@ -266,20 +275,6 @@
     used = lax.broadcasted_iota(jnp.int32, (1, PLANE), 1) < count[0]
     lists[0:1, :] = jnp.where(used, lower[...], -1)
     lists[1:2, :] = jnp.where(used, upper[...], -1)
-    pl.semaphore_wait(barrier, subs + 1)
-    for c in ORDER[:AHEAD]:
-        send_basis(c)
-    odd_copy.wait()
-    for c in ORDER:
-        for q in range(4):
-            at = c * CHUNK + q * PIECE
-            pair = [odd_rows[0:1, at + h * HALF : at + (h + 1) * HALF].astype(jnp.float32) for h in range(2)]
-            extra[c, q] = jnp.concatenate(pair, axis=0).astype(jnp.bfloat16)
-    for c in ORDER:
-        for x, half in enumerate(halves):
-            rb[c, x, 0] = extra[c, 2 * x + half]
-    for c in ORDER[:AHEAD]:
-        send_extra(c)
     list_copy.start()
     sums = (square_a, residual_a, square_b, residual_b)
     for ref in sums:
@@ -297,31 +292,32 @@
             outs = []
             for h in range(2):
                 at = pl.ds(h * HALF, HALF)
-                parts = [ra[c, x, g, :, :, at].reshape(16, HALF) for g in range(3)]
                 odd = jnp.concatenate(
-                    [rb[c, x, q].astype(jnp.float32) for q in range(2)] + [jnp.zeros((12, HALF), jnp.float32)], axis=0
+                    [rb[x, q, c].astype(jnp.float32) for q in range(2)] + [jnp.zeros((12, HALF), jnp.float32)], axis=0
                 )
-                stack = jnp.concatenate([*parts, odd.astype(jnp.bfloat16)], axis=0)
+                stack = jnp.concatenate([ra[c, x, 0, :, at], ra[c, x, 1, :, at], odd.astype(jnp.bfloat16)], axis=0)
                 out = jnp.dot(coefs[x, h], stack, preferred_element_type=jnp.float32)
                 part_a[c, x, :, at] = out[0:16]
-                part_b[c, x, :, at] = out[32:36]
+                part_b[c, x, 4 * h : 4 * h + 4, :] = out[32:36]
                 outs.append(out)
-            send_scaled([out[16:32] for out in outs], to_a.at[c, x])
-            send_scaled([out[36:40] for out in outs], to_b.at[c, x])
+            ends = jnp.concatenate([out[36:40] for out in outs], axis=0)
+            blocks = ([out[16:24] for out in outs], [out[24:32] for out in outs], [ends])
+            send_scaled(blocks, to_sums.at[c, x])
 
     def combine(c):
-        all_of(from_a.at[c], sum_a_sem, c).wait_recv()
-        all_of(from_b.at[c], sum_b_sem, c).wait_recv()
+        all_of(from_sums.at[c], sum_sem, c).wait_recv()
         for x, half in enumerate(halves):
+            got = from_sums.at[c, x]
+            whole = lambda k: got[:, k * HALF : (k + 1) * HALF].astype(jnp.int32).astype(jnp.float32)
+            scale = jnp.exp2(got[:, 5 * HALF : 5 * HALF + 128].astype(jnp.int32).astype(jnp.float32)) * (1.0 / STEPS)
+            ends = (part_b[c, x] + whole(4) * scale[:, 2:3]).astype(jnp.bfloat16)
             for h in range(2):
                 at = pl.ds(h * HALF, HALF)
-                here = pl.ds(pl.multiple_of(c * CHUNK + x * PLANE + half * PIECE + h * HALF, HALF), HALF)
-                vecs = (part_a[c, x, :, at] + scaled_back(from_a.at[c, x], h)).astype(jnp.bfloat16)
-                ea[:, here] = vecs[:8]
-                mate_a[c, x, :, at] = vecs[8:]
-                vecs = (part_b[c, x, :, at] + scaled_back(from_b.at[c, x], h)).astype(jnp.bfloat16)
-                eb[:, here] = vecs[:2]
-                mate_b[c, x, :, at] = vecs[2:]
+                here = pl.ds(pl.multiple_of(c * CHUNK + x * CHUNK // 2 + half * PIECE + h * HALF, HALF), HALF)
+                ea[:, here] = (part_a[c, x, :8, at] + whole(h) * scale[:, 0:1]).astype(jnp.bfloat16)
+                mate_a[c, x, :, at] = (part_a[c, x, 8:, at] + whole(2 + h) * scale[:, 1:2]).astype(jnp.bfloat16)
+                eb[:, here] = ends[4 * h : 4 * h + 2]
+                mate_b[c, x, :, at] = ends[4 * h + 2 : 4 * h + 4]
         send_vecs(c)
 
     def arrived(c):
@@ -344,30 +340,41 @@
         planes_done(0, 1, (first_a, first_b))
         planes_done(rows_local // PLANE - 1, 1, (last_a, last_b))
 
-    later = {6: first_links, 7: last_links}
-    for i, c in enumerate(ORDER):
-        basis_arrived(c)
-        product(c)
-        send_sums(c)
-        if i + AHEAD < len(ORDER):
-            send_basis(ORDER[i + AHEAD])
-            send_extra(ORDER[i + AHEAD])
-        if i >= 1:
-            combine(ORDER[i - 1])
-        if i >= 3:
-            arrived(ORDER[i - 3])
-            if i >= 5:
-                planes_done(2 * ORDER[i - 3] - 1, 2)
+    later = {4: first_links, 5: last_links}
+    depth = rows_local // PLANE
+    present, waiting = set(), list(range(1, depth - 1))
+
+    def settle(i):
+        c = ORDER[i]
+        arrived(c)
+        present.update(range(c * CHUNK // PLANE, (c + 1) * CHUNK // PLANE))
+        ready = [z for z in waiting if {z - 1, z, z + 1} <= present]
+        while ready:
+            n = 1
+            while n < len(ready) and ready[n] == ready[0] + n:
+                n += 1
+            planes_done(ready[0], n)
+            for z in ready[:n]:
+                waiting.remove(z)
+            ready = ready[n:]
+
+    last = len(ORDER)
+    all_of(rb.at[:, 1], extra_sem).wait_recv()
+    for i in range(last + VECS_LAG):
+        if i < last:
+            basis_arrived(ORDER[i])
+            product(ORDER[i])
+            send_sums(ORDER[i])
+            if i + AHEAD < last:
+                send_basis(ORDER[i + AHEAD])
+        if 0 <= i - SUMS_LAG < last:
+            combine(ORDER[i - SUMS_LAG])
         if i in later:
             later[i]()
-    combine(ORDER[-1])
-    outer_planes()
-    arrived(ORDER[-3])
-    planes_done(2 * ORDER[-3] - 1, 2)
-    arrived(ORDER[-2])
-    planes_done(2 * ORDER[-2] - 1, 2)
-    arrived(ORDER[-1])
-    planes_done(2 * ORDER[-1] - 1, 4)
+        if i == OUTER:
+            outer_planes()
+        if i >= VECS_LAG:
+            settle(i - VECS_LAG)
 
     lane = lax.broadcasted_iota(jnp.int32, (1, 128), 1)
     message = jnp.zeros((1, 128), jnp.float32)
@@ -385,10 +392,9 @@
         for copy in copies:
             copy.wait_send()
     list_copy.wait_send()
-    all_of(ra.at[:, :, :, 1], basis_sem).wait_send()
-    all_of(rb.at[:, :, 1], extra_sem).wait_send()
-    all_of(from_a, sum_a_sem).wait_send()
-    all_of(from_b, sum_b_sem).wait_send()
+    all_of(ra.at[:, :, 1], basis_sem).wait_send()
+    all_of(rb.at[:, 1], extra_sem).wait_send()
+    all_of(from_sums, sum_sem).wait_send()
     all_of(mate_a, vec_a_sem).wait_send()
     all_of(mate_b, vec_b_sem).wait_send()
     every = squares.at[pl.ds(0, subs - 1)]
@@ -419,15 +425,15 @@
         out_specs=(vmem,) * 3,
         scratch_shapes=[
             *[pltpu.VMEM(a.shape, a.dtype) for a in arrays[1:]], pltpu.VMEM((2, PLANE), jnp.int32),
-            bf16(1, rows), bf16(chunks, 4, 2, HALF), bf16(2, 2, 40, 64), bf16(8, rows), bf16(2, rows),
+            bf16(1, rows), bf16(2, 2, chunks, 2, HALF), bf16(2, 2, 40, 64), bf16(8, rows), bf16(2, rows),
             bf16(8, PLANE), bf16(2, PLANE), bf16(8, PLANE), bf16(2, PLANE), pltpu.VMEM((2, PLANE), jnp.int32),
-            bf16(chunks, 2, 3, 2, 8, PIECE), bf16(chunks, 2, 2, 2, HALF),
-            f32(chunks, 2, 16, PIECE), f32(chunks, 2, 4, PIECE),
-            *[pltpu.VMEM((chunks, 2, r, PIECE + 128), jnp.int16) for r in (16, 4, 16, 4)],
+            bf16(chunks, 2, 2, 24, PIECE), bf16(2, 2, chunks, 2, HALF),
+            f32(chunks, 2, 16, PIECE), f32(chunks, 2, 8, HALF),
+            *[pltpu.VMEM((chunks, 2, 8, 5 * HALF + 128), jnp.int16) for _ in range(2)],
             bf16(chunks, 2, 8, PIECE), bf16(chunks, 2, 2, PIECE),
             f32(8, PLANE), f32(2, PLANE), f32(8, PLANE), f32(2, PLANE),
             f32(8, 128), f32(8, 128), f32(2, 128), f32(2, 128), f32(subs, 1, 128),
-            dma((7,)), dma((chunks,)), dma(()), dma((7,)), dma((6, chunks)), dma((2, 5)), dma((1,)),
+            dma((7,)), dma((chunks,)), dma(()), dma((6,)), dma((5, chunks)), dma((2, 5)), dma((1,)),
         ],
         compiler_params=pltpu.CompilerParams(
             collective_id=0, has_side_effects=True, vmem_limit_bytes=LIMIT

time: 70.8 us -> 67.9 us (0.959)
  Pallas kernels: 66.2 us -> 63.3 us
    pallas_call x1, Pallas kernels: 66.2 us -> 63.3 us  [whole(): pl.pallas_call(whole_kernel, out_shape=(jax.ShapeDtypeStruct((10, rows),...]
where the time goes in v7:
time: 67.9 us; the launch traced here: 67.8 us
  Pallas kernels  63.3 us (93%)
  local copies, waits for them, and re-layouts  3.15 us (5%)
  between operations  1.29 us (2%)
    pallas_call x1, Pallas kernels, whole(): pl.pallas_call(whole_kernel, out_shape=(jax.ShapeDtypeStruct((10, rows),...  63.3 us
    unnamed x3, local copies, waits for them, and re-layouts  3.15 us

profile of v7, /device:TPU:1, one launch (start us, length us, event | category | flops | bytes accessed | tf_op | source)
XLA Modules:
  0.0 67.8 jit_solution(14477576199963117528)
XLA Ops:
  1.3 63.3 %whole.1 = (bf16[10,65536]{1,0:T(8,128)(2,1)S(1)}, bf16[10,65536]{1,0:T(8,128)(2,1)S(1)}, f32[1,10]{1,0:T(1,128)S(1)}) custom-call(s32[1]{0:T(128)S(6)} %copy.15.count, bf16[25,65536]{1,0:T(8,128)(2,1)} %basis.1, bf16[40,100]{1,0:T(8,128)(2,1)} %bitcast.10, s32[1,4096]{1,0:T(1,128)} %lower_in.1, s32[1,4096]{1,0:T(1,128)} %upper_in.1, f32[1,65536]{1,0:T(1,128)} %bitcast.7, ...), custom_call_target="tpu_custom_call" | custom-call | tf_op jit(solution)/shard_map/whole/pallas_call | solution.py:417
  64.6 1.3 %copy.16 = bf16[10,65536]{1,0:T(8,128)(2,1)} copy(bf16[10,65536]{1,0:T(8,128)(2,1)S(1)} %get-tuple-element.12) | data formatting | bytes 2621440
  65.9 1.3 %copy.17 = bf16[10,65536]{1,0:T(8,128)(2,1)} copy(bf16[10,65536]{1,0:T(8,128)(2,1)S(1)} %get-tuple-element.13) | data formatting | bytes 2621440
  67.2 0.5 copy.18

commit v8 on v7

--- a/solution.py
+++ b/solution.py
@@ -365,10 +365,10 @@
             basis_arrived(ORDER[i])
             product(ORDER[i])
             send_sums(ORDER[i])
-            if i + AHEAD < last:
-                send_basis(ORDER[i + AHEAD])
         if 0 <= i - SUMS_LAG < last:
             combine(ORDER[i - SUMS_LAG])
+        if i + AHEAD < last:
+            send_basis(ORDER[i + AHEAD])
         if i in later:
             later[i]()
         if i == OUTER:
@@ -442,12 +442,36 @@
     )(count, *[pltpu.with_memory_space_constraint(a, pltpu.HBM) for a in arrays])
 
 
+def store_kernel(*refs):
+    sources, targets, sems = refs[:3], refs[3:6], refs[6]
+    copies = [
+        pltpu.make_async_copy(source, target, sems.at[k]) for k, (source, target) in enumerate(zip(sources, targets))
+    ]
+    for copy in copies:
+        copy.start()
+    for copy in copies:
+        copy.wait()
+
+
+def store(*arrays):
+    return pl.pallas_call(
+        store_kernel,
+        out_shape=tuple(jax.ShapeDtypeStruct(a.shape, a.dtype) for a in arrays),
+        in_specs=[pl.BlockSpec(memory_space=pltpu.VMEM)] * 3,
+        out_specs=(pl.BlockSpec(memory_space=pltpu.HBM),) * 3,
+        scratch_shapes=[pltpu.SemaphoreType.DMA((3,))],
+        compiler_params=pltpu.CompilerParams(vmem_limit_bytes=16 * 2**20),
+        name="store",
+    )(*arrays)
+
+
 def on_device(basis, coefficients, eigen_values, stiffness, damping, mass, link_count, lower_cells, upper_cells):
     rows_local = basis.shape[1]
     wide = lambda a: a.reshape(1, rows_local)
     eig, res, norms = whole(
         link_count, basis, coefficients.T, lower_cells, upper_cells, wide(mass), wide(damping), wide(stiffness), eigen_values[None, :]
     )
+    eig, res, norms = store(eig, res, norms)
     return eig, res, norms.reshape(10)
 
 

time: 67.9 us -> 66.5 us (0.979)
  local copies, waits for them, and re-layouts: 3.15 us -> 0 us
  Pallas kernels: 63.3 us -> 65.1 us
    unnamed x3 -> x0, local copies, waits for them, and re-layouts: 3.15 us -> none
    pallas_call x0 -> x1, Pallas kernels: none -> 2.04 us  [store(): pl.pallas_call(store_kernel, out_shape=tuple((jax.ShapeDtypeStruct(a.shap...]
where the time goes in v8:
time: 66.5 us; the launch traced here: 66.3 us
  Pallas kernels  65.1 us (98%)
  between operations  1.29 us (2%)
    pallas_call x1, Pallas kernels, whole(): pl.pallas_call(whole_kernel, out_shape=(jax.ShapeDtypeStruct((10, rows),...  63 us
    pallas_call x1, Pallas kernels, store(): pl.pallas_call(store_kernel, out_shape=tuple((jax.ShapeDtypeStruct(a.shap...  2.04 us

profile of v8, /device:TPU:1, one launch (start us, length us, event | category | flops | bytes accessed | tf_op | source)
XLA Modules:
  0.0 66.3 jit_solution(4596382315282512647)
XLA Ops:
  1.3 63.0 %whole.1 = (bf16[10,65536]{1,0:T(8,128)(2,1)S(1)}, bf16[10,65536]{1,0:T(8,128)(2,1)S(1)}, f32[1,10]{1,0:T(1,128)S(1)}) custom-call(s32[1]{0:T(128)S(6)} %copy.12.count, bf16[25,65536]{1,0:T(8,128)(2,1)} %basis.1, bf16[40,100]{1,0:T(8,128)(2,1)} %bitcast.9, s32[1,4096]{1,0:T(1,128)} %lower_in.1, s32[1,4096]{1,0:T(1,128)} %upper_in.1, f32[1,65536]{1,0:T(1,128)} %bitcast.6, ...), custom_call_target="tpu_custom_call" | custom-call | tf_op jit(solution)/shard_map/whole/pallas_call | solution.py:417
  64.3 2.0 %store.1 = (bf16[10,65536]{1,0:T(8,128)(2,1)}, bf16[10,65536]{1,0:T(8,128)(2,1)}, f32[1,10]{1,0:T(1,128)}) custom-call(bf16[10,65536]{1,0:T(8,128)(2,1)S(1)} %get-tuple-element.9.refs_0_, bf16[10,65536]{1,0:T(8,128)(2,1)S(1)} %get-tuple-element.10.refs_1_, f32[1,10]{1,0:T(1,128)S(1)} %get-tuple-element.11.refs_2_), custom_call_target="tpu_custom_call" | custom-call | tf_op jit(solution)/shard_map/store/pallas_call | solution.py:457

commit v9 on v8

--- a/solution.py
+++ b/solution.py
@@ -9,8 +9,8 @@
 
 WID = 64
 PLANE = WID * WID
-SPAN = 1024
-SLOTS = 512
+SPAN = 2048
+SLOTS = 1024
 LOW = 256
 
 
@@ -94,7 +94,7 @@
             done += [vector_sq, residual_sq]
         return tuple(done)
 
-    totals = lax.fori_loop(0, planes * spans, step, tuple(ref[...] for ref in sums))
+    totals = lax.fori_loop(0, planes * spans, step, tuple(ref[...] for ref in sums), unroll=2)
     for ref, total in zip(sums, totals):
         ref[...] = total
 

time: 66.5 us -> 65.1 us (0.979)
  Pallas kernels: 65.1 us -> 63.7 us
    pallas_call x1, Pallas kernels: 63 us -> 61.6 us  [whole(): pl.pallas_call(whole_kernel, out_shape=(jax.ShapeDtypeStruct((10, rows),...]
where the time goes in v9:
time: 65.1 us; the launch traced here: 65 us
  Pallas kernels  63.7 us (98%)
  between operations  1.29 us (2%)
    pallas_call x1, Pallas kernels, whole(): pl.pallas_call(whole_kernel, out_shape=(jax.ShapeDtypeStruct((10, rows),...  61.6 us
    pallas_call x1, Pallas kernels, store(): pl.pallas_call(store_kernel, out_shape=tuple((jax.ShapeDtypeStruct(a.shap...  2.04 us

profile of v9, /device:TPU:1, one launch (start us, length us, event | category | flops | bytes accessed | tf_op | source)
XLA Modules:
  0.0 65.0 jit_solution(8413808295292788707)
XLA Ops:
  1.3 61.6 %whole.1 = (bf16[10,65536]{1,0:T(8,128)(2,1)S(1)}, bf16[10,65536]{1,0:T(8,128)(2,1)S(1)}, f32[1,10]{1,0:T(1,128)S(1)}) custom-call(s32[1]{0:T(128)S(6)} %copy.12.count, bf16[25,65536]{1,0:T(8,128)(2,1)} %basis.1, bf16[40,100]{1,0:T(8,128)(2,1)} %bitcast.9, s32[1,4096]{1,0:T(1,128)} %lower_in.1, s32[1,4096]{1,0:T(1,128)} %upper_in.1, f32[1,65536]{1,0:T(1,128)} %bitcast.6, ...), custom_call_target="tpu_custom_call" | custom-call | tf_op jit(solution)/shard_map/whole/pallas_call | solution.py:417
  62.9 2.0 %store.1 = (bf16[10,65536]{1,0:T(8,128)(2,1)}, bf16[10,65536]{1,0:T(8,128)(2,1)}, f32[1,10]{1,0:T(1,128)}) custom-call(bf16[10,65536]{1,0:T(8,128)(2,1)S(1)} %get-tuple-element.9.refs_0_, bf16[10,65536]{1,0:T(8,128)(2,1)S(1)} %get-tuple-element.10.refs_1_, f32[1,10]{1,0:T(1,128)S(1)} %get-tuple-element.11.refs_2_), custom_call_target="tpu_custom_call" | custom-call | tf_op jit(solution)/shard_map/store/pallas_call | solution.py:457

commit v10 on v9

--- a/solution.py
+++ b/solution.py
@@ -163,7 +163,7 @@
     odd_rows, extra, coefs, ea, eb, above_a, above_b, below_a, below_b, down_lists, ra, rb,
     part_a, part_b, to_sums, from_sums, mate_a, mate_b,
     first_a, first_b, last_a, last_b, square_a, residual_a, square_b, residual_b, squares,
-    input_sem, own_sem, odd_sem, sent_sem, chunk_sem, plane_sem, square_recv_sem,
+    input_sem, own_sem, odd_sem, sent_sem, chunk_sem, extra_recv_sem, plane_sem, square_recv_sem,
 ):
     me, sub = lax.axis_index("vecs"), lax.axis_index("rows")
     subs = lax.axis_size("rows")
@@ -172,7 +172,7 @@
     mates, crosses = (one, two), (two, one)
     halves = (lax.rem(lax.div(me + 1, 2), 2), lax.div(me, 2))
     basis_sem, extra_sem, sum_sem, vec_a_sem, vec_b_sem = (
-        (sent_sem.at[k], chunk_sem.at[k]) for k in range(5)
+        (sent_sem.at[k], extra_recv_sem if k == 1 else chunk_sem.at[k - (k > 1)]) for k in range(5)
     )
     square_sem = (sent_sem.at[5], square_recv_sem)
 
@@ -433,7 +433,7 @@
             bf16(chunks, 2, 8, PIECE), bf16(chunks, 2, 2, PIECE),
             f32(8, PLANE), f32(2, PLANE), f32(8, PLANE), f32(2, PLANE),
             f32(8, 128), f32(8, 128), f32(2, 128), f32(2, 128), f32(subs, 1, 128),
-            dma((7,)), dma((chunks,)), dma(()), dma((6,)), dma((5, chunks)), dma((2, 5)), dma((1,)),
+            dma((7,)), dma((chunks,)), dma(()), dma((6,)), dma((4, chunks)), dma((1,)), dma((2, 5)), dma((1,)),
         ],
         compiler_params=pltpu.CompilerParams(
             collective_id=0, has_side_effects=True, vmem_limit_bytes=LIMIT

time: 65.1 us -> 65 us (level)
  no operation moved by 1% of the time
where the time goes in v10:
time: 65 us; the launch traced here: 64.9 us
  Pallas kernels  63.6 us (98%)
  between operations  1.29 us (2%)
    pallas_call x1, Pallas kernels, whole(): pl.pallas_call(whole_kernel, out_shape=(jax.ShapeDtypeStruct((10, rows),...  61.6 us
    pallas_call x1, Pallas kernels, store(): pl.pallas_call(store_kernel, out_shape=tuple((jax.ShapeDtypeStruct(a.shap...  2.04 us

profile of v10, /device:TPU:1, one launch (start us, length us, event | category | flops | bytes accessed | tf_op | source)
XLA Modules:
  0.0 64.9 jit_solution(16166350183708083531)
XLA Ops:
  1.3 61.6 %whole.1 = (bf16[10,65536]{1,0:T(8,128)(2,1)S(1)}, bf16[10,65536]{1,0:T(8,128)(2,1)S(1)}, f32[1,10]{1,0:T(1,128)S(1)}) custom-call(s32[1]{0:T(128)S(6)} %copy.12.count, bf16[25,65536]{1,0:T(8,128)(2,1)} %basis.1, bf16[40,100]{1,0:T(8,128)(2,1)} %bitcast.9, s32[1,4096]{1,0:T(1,128)} %lower_in.1, s32[1,4096]{1,0:T(1,128)} %upper_in.1, f32[1,65536]{1,0:T(1,128)} %bitcast.6, ...), custom_call_target="tpu_custom_call" | custom-call | tf_op jit(solution)/shard_map/whole/pallas_call | solution.py:417
  62.9 2.0 %store.1 = (bf16[10,65536]{1,0:T(8,128)(2,1)}, bf16[10,65536]{1,0:T(8,128)(2,1)}, f32[1,10]{1,0:T(1,128)}) custom-call(bf16[10,65536]{1,0:T(8,128)(2,1)S(1)} %get-tuple-element.9.refs_0_, bf16[10,65536]{1,0:T(8,128)(2,1)S(1)} %get-tuple-element.10.refs_1_, f32[1,10]{1,0:T(1,128)S(1)} %get-tuple-element.11.refs_2_), custom_call_target="tpu_custom_call" | custom-call | tf_op jit(solution)/shard_map/store/pallas_call | solution.py:457

commit v11 on v10

--- a/solution.py
+++ b/solution.py
@@ -208,10 +208,9 @@
 
     def own_copies(c):
         for x, half in enumerate(halves):
-            yield pltpu.make_async_copy(basis.at[pl.ds(0, 24), columns(c, x, half)], ra.at[c, x, 0], own_sem.at[c])
+            yield pltpu.make_async_copy(basis.at[pl.ds(0, 24), columns(c, x, half)], ra.at[c, x, 0], own_sem)
 
     def basis_arrived(c):
-        pltpu.make_async_copy(ra.at[c, :, 0], ra.at[c, :, 0], own_sem.at[c]).wait()
         all_of(ra.at[c, :, 1], basis_sem, c).wait_recv()
 
     def send_sums(c):
@@ -359,6 +358,7 @@
             ready = ready[n:]
 
     last = len(ORDER)
+    pltpu.make_async_copy(ra.at[:, :, 0], ra.at[:, :, 0], own_sem).wait()
     all_of(rb.at[:, 1], extra_sem).wait_recv()
     for i in range(last + VECS_LAG):
         if i < last:
@@ -433,7 +433,7 @@
             bf16(chunks, 2, 8, PIECE), bf16(chunks, 2, 2, PIECE),
             f32(8, PLANE), f32(2, PLANE), f32(8, PLANE), f32(2, PLANE),
             f32(8, 128), f32(8, 128), f32(2, 128), f32(2, 128), f32(subs, 1, 128),
-            dma((7,)), dma((chunks,)), dma(()), dma((6,)), dma((4, chunks)), dma((1,)), dma((2, 5)), dma((1,)),
+            dma((7,)), dma(()), dma(()), dma((6,)), dma((4, chunks)), dma((1,)), dma((2, 5)), dma((1,)),
         ],
         compiler_params=pltpu.CompilerParams(
             collective_id=0, has_side_effects=True, vmem_limit_bytes=LIMIT

time: 65 us -> 64.9 us (level)
  no operation moved by 1% of the time
where the time goes in v11:
time: 64.9 us; the launch traced here: 64.8 us
  Pallas kernels  63.5 us (98%)
  between operations  1.29 us (2%)
    pallas_call x1, Pallas kernels, whole(): pl.pallas_call(whole_kernel, out_shape=(jax.ShapeDtypeStruct((10, rows),...  61.5 us
    pallas_call x1, Pallas kernels, store(): pl.pallas_call(store_kernel, out_shape=tuple((jax.ShapeDtypeStruct(a.shap...  2.04 us

profile of v11, /device:TPU:1, one launch (start us, length us, event | category | flops | bytes accessed | tf_op | source)
XLA Modules:
  0.0 64.8 jit_solution(1563323352381239096)
XLA Ops:
  1.3 61.5 %whole.1 = (bf16[10,65536]{1,0:T(8,128)(2,1)S(1)}, bf16[10,65536]{1,0:T(8,128)(2,1)S(1)}, f32[1,10]{1,0:T(1,128)S(1)}) custom-call(s32[1]{0:T(128)S(6)} %copy.12.count, bf16[25,65536]{1,0:T(8,128)(2,1)} %basis.1, bf16[40,100]{1,0:T(8,128)(2,1)} %bitcast.9, s32[1,4096]{1,0:T(1,128)} %lower_in.1, s32[1,4096]{1,0:T(1,128)} %upper_in.1, f32[1,65536]{1,0:T(1,128)} %bitcast.6, ...), custom_call_target="tpu_custom_call" | custom-call | tf_op jit(solution)/shard_map/whole/pallas_call | solution.py:417
  62.8 2.0 %store.1 = (bf16[10,65536]{1,0:T(8,128)(2,1)}, bf16[10,65536]{1,0:T(8,128)(2,1)}, f32[1,10]{1,0:T(1,128)}) custom-call(bf16[10,65536]{1,0:T(8,128)(2,1)S(1)} %get-tuple-element.9.refs_0_, bf16[10,65536]{1,0:T(8,128)(2,1)S(1)} %get-tuple-element.10.refs_1_, f32[1,10]{1,0:T(1,128)S(1)} %get-tuple-element.11.refs_2_), custom_call_target="tpu_custom_call" | custom-call | tf_op jit(solution)/shard_map/store/pallas_call | solution.py:457
